TPU v7x, 256 devices: a whole 4x4x8 slice. The times are simulated.
256 devices in a mesh: row: 64 (over y, x, z_hi), ka: 4 (over z_lo, core).
Axes of the slice: x: 4, y: 4, z: 8 (z_hi: 4, z_lo: 2; z = z_hi * 2 + z_lo), core: 2. Of those that a mesh axis runs over, the one named last changes fastest.
Arguments:
- pair_rep: bfloat16 [256, 256, 128], P('row', 'ka'), may hold values from -6 to 6
- in_weights: bfloat16 [2, 128, 512], replicated, may hold values from -0.5 to 0.5
- gate_weights: bfloat16 [2, 128, 128], replicated, may hold values from -0.5 to 0.5
- out_weights: bfloat16 [2, 128, 128], replicated, may hold values from -0.5 to 0.5
Outputs:
- refined: bfloat16 [256, 256, 128], P('row', 'ka')
All inputs are finite; a program needn't handle non-finite values.
Results may differ from a plain program's by a relative error of at most 0.015.
Values may be sent and summed in bfloat16 or wider, within the bound.
No kernel may reach another device: no remote copies, remote signals or barrier semaphores. Data moves between devices by JAX's collectives and lax.ppermute only.
A program may use at most 64 MiB of HBM per device.

v0:
```python
import jax
import jax.numpy as jnp
from jax import lax
from jax.sharding import PartitionSpec as P

EPSILON = 1e-05


def swapped(value, axis, stride):
    mask = 2**stride
    pairs = [(source, source ^ mask) for source in range(lax.axis_size(axis))]
    return lax.ppermute(value, axis, pairs)


def in_blocks(x, dim, size):
    before, after = (x.shape[:dim], x.shape[dim + 1 :])
    return jnp.moveaxis(x.reshape(*before, size, -1, *after), dim, 0)


def sum_at_owner(x, axis, dim):
    size = lax.axis_size(axis)
    tiles = lax.all_to_all(in_blocks(x, dim, size), axis, 0, 0, tiled=True)
    return jnp.sum(tiles.astype(jnp.float32), axis=0)


def side_by_side(arrays, axis, split_dim, concat_dim, along):
    widths = [a.shape[along] for a in arrays]
    both = jnp.concatenate(arrays, axis=along)
    whole = lax.all_to_all(both, axis, split_axis=split_dim, concat_axis=concat_dim, tiled=True)
    return tuple(jnp.split(whole, [sum(widths[:k]) for k in range(1, len(widths))], axis=along))


def normalize(values):
    values = values.astype(jnp.float32)
    centre = jnp.mean(values, axis=-1, keepdims=True)
    shifted = values - centre
    spread = jnp.mean(shifted * shifted, axis=-1, keepdims=True)
    return shifted * lax.rsqrt(spread + EPSILON)


def flatten_normed(blocks):
    normed = normalize(blocks).astype(jnp.bfloat16)
    return normed.reshape(-1, blocks.shape[-1])


def operands(flattened, weights, shape):
    columns = weights.shape[1] // 4
    projected = jnp.dot(flattened, weights, preferred_element_type=jnp.float32)
    left_rows = (
        jax.nn.sigmoid(projected[:, :columns]) * projected[:, columns : 2 * columns]
    ).astype(jnp.bfloat16)
    right_rows = (
        jax.nn.sigmoid(projected[:, 2 * columns : 3 * columns]) * projected[:, 3 * columns :]
    ).astype(jnp.bfloat16)
    return (
        left_rows.reshape(shape[0], shape[1], columns),
        right_rows.reshape(shape[0], shape[1], columns),
    )


def gates(flattened, weights, shape):
    gating = jax.nn.sigmoid(jnp.dot(flattened, weights, preferred_element_type=jnp.float32))
    return gating.reshape(shape[0], shape[1], weights.shape[1])


def bit_of(position):
    return lax.axis_index("row") // (1 << position) % 2


def doubling(values, first, count, fetch):
    for position in range(first, first + count):
        other = fetch(values, position)
        upper = bit_of(position) == 1
        values = jnp.where(
            upper, jnp.concatenate([other, values], 0), jnp.concatenate([values, other], 0)
        )
    return values


def route(arranged, first, count):
    for offset in range(count):
        position = first + offset
        mine = bit_of(position)
        sources, targets = (arranged.shape[0], arranged.shape[1])
        split = arranged.reshape((sources, targets // 2, 2) + arranged.shape[2:])
        keep = lax.dynamic_index_in_dim(split, mine, 2, keepdims=False)
        sent = lax.dynamic_index_in_dim(split, 1 - mine, 2, keepdims=False)
        received = swapped(sent.astype(jnp.bfloat16), "row", position).astype(sent.dtype)
        stacked = jnp.where(
            mine == 1, jnp.stack([received, keep], 0), jnp.stack([keep, received], 0)
        )
        arranged = stacked.reshape((2 * sources, targets // 2) + arranged.shape[2:])
    return arranged


def blocked_partial(left_rows, right_rows):
    levels = lax.axis_size("row").bit_length() - 1
    lower = levels // 3
    upper = levels - lower
    left_all = doubling(
        left_rows, lower, upper, lambda values, position: swapped(values, "row", position)
    )
    right_all = doubling(
        right_rows, 0, lower, lambda values, position: swapped(values, "row", position)
    )
    blocks = jnp.einsum("ikh,jkh->ijh", left_all, right_all, preferred_element_type=jnp.float32)
    height = left_rows.shape[0]
    width = right_all.shape[0]
    channels = blocks.shape[-1]
    blocks = blocks.reshape(1, 1 << upper, height, width, channels)
    routed = route(blocks, lower, upper)
    routed = routed.reshape(1 << upper, height, width, channels)
    return jnp.transpose(routed, (1, 0, 2, 3)).reshape(height, (1 << upper) * width, channels)


def triangle(left_rows, right_rows):
    partial_value = blocked_partial(left_rows, right_rows)
    return sum_at_owner(partial_value.astype(jnp.bfloat16), "ka", 1)


def finish(state, gating, product, weights):
    squeezed = normalize(product).astype(jnp.bfloat16).reshape(-1, product.shape[-1])
    update = jnp.dot(squeezed, weights, preferred_element_type=jnp.float32).reshape(gating.shape)
    return (state.astype(jnp.float32) + gating * update).astype(jnp.bfloat16)


def per_device(pair_rep, in_weights, gate_weights, out_weights):
    shape = pair_rep.shape
    flattened = flatten_normed(pair_rep)
    left_rows, right_rows = operands(flattened, in_weights[0], shape)
    gating = gates(flattened, gate_weights[0], shape)
    middle = finish(pair_rep, gating, triangle(left_rows, right_rows), out_weights[0])
    flat_middle = flatten_normed(middle)
    left_near, right_near = operands(flat_middle, in_weights[1], shape)
    gating_far = gates(flat_middle, gate_weights[1], shape)
    left_far, right_far = side_by_side(
        (jnp.swapaxes(left_near, 0, 1), jnp.swapaxes(right_near, 0, 1)), "ka", 1, 0, 2
    )
    left_far, right_far = side_by_side((left_far, right_far), "row", 0, 1, 2)
    return finish(middle, gating_far, triangle(left_far, right_far), out_weights[1])


def solution(mesh):
    in_specs = (P("row", "ka", None), P(), P(), P())
    out_specs = P("row", "ka", None)
    return jax.shard_map(
        per_device, mesh=mesh, in_specs=in_specs, out_specs=out_specs, check_vma=False
    )
```

profile of v0, /device:TPU:1, one launch (start us, length us, event | category | flops | bytes accessed | tf_op | source)
XLA Modules:
  0.0 201.3 jit_solution(13104829864049712605)
XLA Ops:
  0.0 0.9 convert_reduce_fusion.4
  1.0 1.0 fusion.15
  2.0 1.0 fusion.16
  3.0 1.1 fusion.43
  4.2 2.1 %collective-permute-start.2 = (bf16[4,64,128]{2,0,1:T(4,128)(2,1)S(1)}, bf16[4,64,128]{2,0,1:T(4,128)(2,1)S(1)}, u32[]{:S(2)}, u32[]{:S(2)}) collective-permute-start(bf16[4,64,128]{2,0,1:T(4,128)(2,1)S(1)} %copy.79), channel_id=1, source_target_pairs={{0,16},{4,20},{8,24},{12,28},{16,0},{20,4},{24,8},{28,12},{32,48},... | collective-permute-start | bytes 196616 | tf_op jit(solution)/shard_map/ppermute | solution.py:12
  6.4 1.7 collective-permute-done.2
  8.1 3.1 %collective-permute-start.3 = (bf16[8,64,128]{2,0,1:T(8,128)(2,1)S(1)}, bf16[8,64,128]{2,0,1:T(8,128)(2,1)S(1)}, u32[]{:S(2)}, u32[]{:S(2)}) collective-permute-start(bf16[8,64,128]{2,0,1:T(8,128)(2,1)S(1)} %maximum_select_fusion.17), channel_id=1, source_target_pairs={{0,32},{4,36},{8,40},{12,44},{16,48},{20,52},{24,56},{28,60},{32,0... | collective-permute-start | bytes 393224 | tf_op jit(solution)/shard_map/ppermute | solution.py:12
  11.2 2.4 %collective-permute-done.3 = bf16[8,64,128]{2,0,1:T(8,128)(2,1)S(1)} collective-permute-done((bf16[8,64,128]{2,0,1:T(8,128)(2,1)S(1)}, bf16[8,64,128]{2,0,1:T(8,128)(2,1)S(1)}, u32[]{:S(2)}, u32[]{:S(2)}) %collective-permute-start.3) | collective-permute-done | bytes 131104 | tf_op jit(solution)/shard_map/ppermute | solution.py:12
  13.7 1.6 collective-permute-start.4
  15.3 3.8 %collective-permute-done.4 = bf16[16,64,128]{2,0,1:T(8,128)(2,1)S(1)} collective-permute-done((bf16[16,64,128]{2,0,1:T(8,128)(2,1)S(1)}, bf16[16,64,128]{2,0,1:T(8,128)(2,1)S(1)}, u32[]{:S(2)}, u32[]{:S(2)}) %collective-permute-start.4) | collective-permute-done | bytes 262176 | tf_op jit(solution)/shard_map/ppermute | solution.py:12
  19.2 3.2 %collective-permute-start.5 = (bf16[32,64,128]{2,0,1:T(8,128)(2,1)S(1)}, bf16[32,64,128]{2,0,1:T(8,128)(2,1)S(1)}, u32[]{:S(2)}, u32[]{:S(2)}) collective-permute-start(bf16[32,64,128]{2,0,1:T(8,128)(2,1)S(1)} %maximum_select_fusion.2), channel_id=1, source_target_pairs={{0,128},{4,132},{8,136},{12,140},{16,144},{20,148},{24,152},{28,15... | collective-permute-start | bytes 1572872 | tf_op jit(solution)/shard_map/ppermute | solution.py:12
  22.4 3.1 %collective-permute-start = (bf16[4,64,128]{2,0,1:T(4,128)(2,1)S(1)}, bf16[4,64,128]{2,0,1:T(4,128)(2,1)S(1)}, u32[]{:S(2)}, u32[]{:S(2)}) collective-permute-start(bf16[4,64,128]{2,0,1:T(4,128)(2,1)S(1)} %copy.76), channel_id=1, source_target_pairs={{0,4},{4,0},{8,12},{12,8},{16,20},{20,16},{24,28},{28,24},{32,36},... | collective-permute-start | bytes 196616 | tf_op jit(solution)/shard_map/ppermute | solution.py:12
  25.5 1.7 collective-permute-done
  27.3 7.1 %collective-permute-start.1 = (bf16[8,64,128]{2,0,1:T(8,128)(2,1)S(1)}, bf16[8,64,128]{2,0,1:T(8,128)(2,1)S(1)}, u32[]{:S(2)}, u32[]{:S(2)}) collective-permute-start(bf16[8,64,128]{2,0,1:T(8,128)(2,1)S(1)} %maximum_select_fusion.16), channel_id=1, source_target_pairs={{0,8},{4,12},{8,0},{12,4},{16,24},{20,28},{24,16},{28,20},{32,40},... | collective-permute-start | bytes 393224 | tf_op jit(solution)/shard_map/ppermute | solution.py:12
  34.3 2.5 %collective-permute-done.1 = bf16[8,64,128]{2,0,1:T(8,128)(2,1)S(1)} collective-permute-done((bf16[8,64,128]{2,0,1:T(8,128)(2,1)S(1)}, bf16[8,64,128]{2,0,1:T(8,128)(2,1)S(1)}, u32[]{:S(2)}, u32[]{:S(2)}) %collective-permute-start.1) | collective-permute-done | bytes 131104 | tf_op jit(solution)/shard_map/ppermute | solution.py:12
  36.9 1.3 copy.82
  38.5 3.5 %copy.83 = bf16[64,64,128]{1,0,2:T(8,128)(2,1)S(1)} copy(bf16[64,64,128]{2,0,1:T(8,128)(2,1)S(1)} %maximum_select_fusion) | data formatting | bytes 2097152 | tf_op jit(solution)/shard_map/jit(_where)/select_n | solution.py:74
  42.1 2.2 %convolution_bitcast_fusion.1 = bf16[64,16,128]{0,1,2:T(8,128)(2,1)S(1)} fusion(bf16[16,64,128]{1,0,2:T(8,128)(2,1)} %copy.82, bf16[64,64,128]{1,0,2:T(8,128)(2,1)S(1)} %copy.83), kind=kOutput, calls=%fused_computation.1 | convolution fusion | flops 16777216 | bytes 1572864 | tf_op jit(solution)/shard_map/ikh,jkh->ijh/dot_general | solution.py:106
  44.9 1.3 collective-permute-start.6
  46.2 2.6 %collective-permute-done.6 = bf16[1,8,4,16,128]{4,3,2,1,0:T(8,128)(2,1)S(1)} collective-permute-done((bf16[1,8,4,16,128]{4,3,2,1,0:T(8,128)(2,1)S(1)}, bf16[1,8,4,16,128]{4,3,2,1,0:T(8,128)(2,1)S(1)}, u32[]{:S(2)}, u32[]{:S(2)}) %collective-permute-start.6) | collective-permute-done | bytes 131104 | tf_op jit(solution)/shard_map/ppermute | solution.py:12
  48.9 2.8 %collective-permute-start.7 = (bf16[2,4,4,16,128]{4,3,2,1,0:T(8,128)(2,1)S(1)}, bf16[2,4,4,16,128]{4,3,2,1,0:T(8,128)(2,1)S(1)}, u32[]{:S(2)}, u32[]{:S(2)}) collective-permute-start(bf16[2,4,4,16,128]{4,3,2,1,0:T(8,128)(2,1)S(1)} %get-tuple-element.25), channel_id=1, source_target_pairs={{0,32},{4,36},{8,40},{12,44},{16,48},{20,52},{24,56},{28,60},{32,0... | collective-permute-start | bytes 393224 | tf_op jit(solution)/shard_map/ppermute | solution.py:12
  51.7 2.6 %collective-permute-done.7 = bf16[2,4,4,16,128]{4,3,2,1,0:T(8,128)(2,1)S(1)} collective-permute-done((bf16[2,4,4,16,128]{4,3,2,1,0:T(8,128)(2,1)S(1)}, bf16[2,4,4,16,128]{4,3,2,1,0:T(8,128)(2,1)S(1)}, u32[]{:S(2)}, u32[]{:S(2)}) %collective-permute-start.7) | collective-permute-done | bytes 131104 | tf_op jit(solution)/shard_map/ppermute | solution.py:12
  54.8 3.4 %collective-permute-done.8 = bf16[4,2,4,16,128]{4,3,2,1,0:T(8,128)(2,1)S(1)} collective-permute-done((bf16[4,2,4,16,128]{4,3,2,1,0:T(8,128)(2,1)S(1)}, bf16[4,2,4,16,128]{4,3,2,1,0:T(8,128)(2,1)S(1)}, u32[]{:S(2)}, u32[]{:S(2)}) %collective-permute-start.8) | collective-permute-done | bytes 131104 | tf_op jit(solution)/shard_map/ppermute | solution.py:12
  58.9 5.0 %collective-permute-done.9 = bf16[8,1,4,16,128]{4,3,2,0,1:T(8,128)(2,1)S(1)} collective-permute-done((bf16[8,1,4,16,128]{4,3,2,0,1:T(8,128)(2,1)S(1)}, bf16[8,1,4,16,128]{4,3,2,0,1:T(8,128)(2,1)S(1)}, u32[]{:S(2)}, u32[]{:S(2)}) %collective-permute-start.9) | collective-permute-done | bytes 131104 | tf_op jit(solution)/shard_map/ppermute | solution.py:12
  64.0 0.7 copy.88
  64.8 15.9 %all-to-all-start = ((bf16[4,4,64,128]{3,2,1,0:T(8,128)(2,1)}), bf16[4,4,64,128]{3,2,1,0:T(8,128)(2,1)S(1)}, u32[]{:S(2)}, u32[]{:S(2)}) async-start(bf16[4,4,64,128]{3,2,1,0:T(8,128)(2,1)} %copy.88), calls=%async_computation | async-start | bytes 524288 | tf_op jit(solution)/shard_map/all_to_all | solution.py:22
  80.8 4.9 %all-to-all-done = bf16[4,4,64,128]{3,2,1,0:T(8,128)(2,1)S(1)} async-done(((bf16[4,4,64,128]{3,2,1,0:T(8,128)(2,1)}), bf16[4,4,64,128]{3,2,1,0:T(8,128)(2,1)S(1)}, u32[]{:S(2)}, u32[]{:S(2)}) %all-to-all-start) | async-done | bytes 262176 | tf_op jit(solution)/shard_map/all_to_all | solution.py:22
  87.0 6.9 %all_to_all.46 = bf16[64,4,256]{2,0,1:T(8,128)(2,1)S(1)} all-to-all(bf16[64,4,256]{2,0,1:T(8,128)(2,1)S(1)} %pad_maximum_fusion), channel_id=1, replica_groups=mesh['row'=64,'ka'=4] {'ka'}, dimensions={1} | all-to-all | bytes 262144 | tf_op jit(solution)/shard_map/all_to_all | solution.py:29
  95.2 23.7 %all_to_all.47 = bf16[64,2,512]{2,1,0:T(2,128)(2,1)S(1)} all-to-all(bf16[64,2,512]{2,1,0:T(2,128)(2,1)S(1)} %reshape.355), channel_id=1, replica_groups=mesh['row'=64,'ka'=4] {'row'}, dimensions={0} | all-to-all | bytes 262144 | tf_op jit(solution)/shard_map/all_to_all | solution.py:29
  119.0 0.8 reduce.2
  120.3 2.8 %collective-permute-done.12 = bf16[4,64,128]{2,0,1:T(4,128)(2,1)S(1)} collective-permute-done((bf16[4,64,128]{2,0,1:T(4,128)(2,1)S(1)}, bf16[4,64,128]{2,0,1:T(4,128)(2,1)S(1)}, u32[]{:S(2)}, u32[]{:S(2)}) %collective-permute-start.12) | collective-permute-done | bytes 65568 | tf_op jit(solution)/shard_map/ppermute | solution.py:12
  123.6 5.0 %collective-permute-done.13 = bf16[8,64,128]{2,0,1:T(8,128)(2,1)S(1)} collective-permute-done((bf16[8,64,128]{2,0,1:T(8,128)(2,1)S(1)}, bf16[8,64,128]{2,0,1:T(8,128)(2,1)S(1)}, u32[]{:S(2)}, u32[]{:S(2)}) %collective-permute-start.13) | collective-permute-done | bytes 131104 | tf_op jit(solution)/shard_map/ppermute | solution.py:12
  129.3 4.7 %collective-permute-done.14 = bf16[16,64,128]{2,0,1:T(8,128)(2,1)S(1)} collective-permute-done((bf16[16,64,128]{2,0,1:T(8,128)(2,1)S(1)}, bf16[16,64,128]{2,0,1:T(8,128)(2,1)S(1)}, u32[]{:S(2)}, u32[]{:S(2)}) %collective-permute-start.14) | collective-permute-done | bytes 262176 | tf_op jit(solution)/shard_map/ppermute | solution.py:12
  135.0 4.5 %collective-permute-done.10 = bf16[4,64,128]{2,0,1:T(4,128)(2,1)S(1)} collective-permute-done((bf16[4,64,128]{2,0,1:T(4,128)(2,1)S(1)}, bf16[4,64,128]{2,0,1:T(4,128)(2,1)S(1)}, u32[]{:S(2)}, u32[]{:S(2)}) %collective-permute-start.10) | collective-permute-done | bytes 65568 | tf_op jit(solution)/shard_map/ppermute | solution.py:12
  139.6 1.2 collective-permute-start.11
  140.8 8.8 %collective-permute-done.11 = bf16[8,64,128]{2,0,1:T(8,128)(2,1)S(1)} collective-permute-done((bf16[8,64,128]{2,0,1:T(8,128)(2,1)S(1)}, bf16[8,64,128]{2,0,1:T(8,128)(2,1)S(1)}, u32[]{:S(2)}, u32[]{:S(2)}) %collective-permute-start.11) | collective-permute-done | bytes 131104 | tf_op jit(solution)/shard_map/ppermute | solution.py:12
  149.6 1.3 copy.90
  151.3 3.5 %copy.91 = bf16[64,64,128]{1,0,2:T(8,128)(2,1)S(1)} copy(bf16[64,64,128]{2,0,1:T(8,128)(2,1)S(1)} %maximum_select_fusion.1) | data formatting | bytes 2097152 | tf_op jit(solution)/shard_map/jit(_where)/select_n | solution.py:74
  154.8 2.2 %convolution_bitcast_fusion = bf16[64,16,128]{0,1,2:T(8,128)(2,1)S(1)} fusion(bf16[16,64,128]{1,0,2:T(8,128)(2,1)} %copy.90, bf16[64,64,128]{1,0,2:T(8,128)(2,1)S(1)} %copy.91), kind=kOutput, calls=%fused_computation | convolution fusion | flops 16777216 | bytes 1572864 | tf_op jit(solution)/shard_map/ikh,jkh->ijh/dot_general | solution.py:106
  158.1 3.5 %collective-permute-done.16 = bf16[1,8,4,16,128]{4,3,2,1,0:T(8,128)(2,1)S(1)} collective-permute-done((bf16[1,8,4,16,128]{4,3,2,1,0:T(8,128)(2,1)S(1)}, bf16[1,8,4,16,128]{4,3,2,1,0:T(8,128)(2,1)S(1)}, u32[]{:S(2)}, u32[]{:S(2)}) %collective-permute-start.16) | collective-permute-done | bytes 131104 | tf_op jit(solution)/shard_map/ppermute | solution.py:12
  162.0 5.0 %collective-permute-done.17 = bf16[2,4,4,16,128]{4,3,2,1,0:T(8,128)(2,1)S(1)} collective-permute-done((bf16[2,4,4,16,128]{4,3,2,1,0:T(8,128)(2,1)S(1)}, bf16[2,4,4,16,128]{4,3,2,1,0:T(8,128)(2,1)S(1)}, u32[]{:S(2)}, u32[]{:S(2)}) %collective-permute-start.17) | collective-permute-done | bytes 131104 | tf_op jit(solution)/shard_map/ppermute | solution.py:12
  167.2 4.1 %collective-permute-done.18 = bf16[4,2,4,16,128]{4,3,2,1,0:T(8,128)(2,1)S(1)} collective-permute-done((bf16[4,2,4,16,128]{4,3,2,1,0:T(8,128)(2,1)S(1)}, bf16[4,2,4,16,128]{4,3,2,1,0:T(8,128)(2,1)S(1)}, u32[]{:S(2)}, u32[]{:S(2)}) %collective-permute-start.18) | collective-permute-done | bytes 131104 | tf_op jit(solution)/shard_map/ppermute | solution.py:12
  171.3 1.6 collective-permute-start.19
  172.9 3.8 %collective-permute-done.19 = bf16[8,1,4,16,128]{4,3,2,0,1:T(8,128)(2,1)S(1)} collective-permute-done((bf16[8,1,4,16,128]{4,3,2,0,1:T(8,128)(2,1)S(1)}, bf16[8,1,4,16,128]{4,3,2,0,1:T(8,128)(2,1)S(1)}, u32[]{:S(2)}, u32[]{:S(2)}) %collective-permute-start.19) | collective-permute-done | bytes 131104 | tf_op jit(solution)/shard_map/ppermute | solution.py:12
  176.8 0.7 copy.96
  177.5 17.5 %all-to-all-start.3 = ((bf16[4,4,64,128]{3,2,1,0:T(8,128)(2,1)}), bf16[4,4,64,128]{3,2,1,0:T(8,128)(2,1)S(1)}, u32[]{:S(2)}, u32[]{:S(2)}) async-start(bf16[4,4,64,128]{3,2,1,0:T(8,128)(2,1)} %copy.96), calls=%async_computation.3 | async-start | bytes 524288 | tf_op jit(solution)/shard_map/all_to_all | solution.py:22
  195.2 4.9 %all-to-all-done.3 = bf16[4,4,64,128]{3,2,1,0:T(8,128)(2,1)S(1)} async-done(((bf16[4,4,64,128]{3,2,1,0:T(8,128)(2,1)}), bf16[4,4,64,128]{3,2,1,0:T(8,128)(2,1)S(1)}, u32[]{:S(2)}, u32[]{:S(2)}) %all-to-all-start.3) | async-done | bytes 262176 | tf_op jit(solution)/shard_map/all_to_all | solution.py:22
  200.4 0.9 fusion.9
  (81 shorter events, 11.4 us)
Async XLA Ops:
  4.2 3.8 %collective-permute-start.2 = (bf16[4,64,128]{2,0,1:T(4,128)(2,1)S(1)}, bf16[4,64,128]{2,0,1:T(4,128)(2,1)S(1)}, u32[]{:S(2)}, u32[]{:S(2)}) collective-permute-start(bf16[4,64,128]{2,0,1:T(4,128)(2,1)S(1)} %copy.79), channel_id=1, source_target_pairs={{0,16},{4,20},{8,24},{12,28},{16,0},{20,4},{24,8},{28,12},{32,48},... | collective-permute-start | bytes 196616 | tf_op jit(solution)/shard_map/ppermute | solution.py:12
  8.1 5.4 %collective-permute-start.3 = (bf16[8,64,128]{2,0,1:T(8,128)(2,1)S(1)}, bf16[8,64,128]{2,0,1:T(8,128)(2,1)S(1)}, u32[]{:S(2)}, u32[]{:S(2)}) collective-permute-start(bf16[8,64,128]{2,0,1:T(8,128)(2,1)S(1)} %maximum_select_fusion.17), channel_id=1, source_target_pairs={{0,32},{4,36},{8,40},{12,44},{16,48},{20,52},{24,56},{28,60},{32,0... | collective-permute-start | bytes 393224 | tf_op jit(solution)/shard_map/ppermute | solution.py:12
  13.7 5.4 %collective-permute-start.4 = (bf16[16,64,128]{2,0,1:T(8,128)(2,1)S(1)}, bf16[16,64,128]{2,0,1:T(8,128)(2,1)S(1)}, u32[]{:S(2)}, u32[]{:S(2)}) collective-permute-start(bf16[16,64,128]{2,0,1:T(8,128)(2,1)S(1)} %maximum_select_fusion.13), channel_id=1, source_target_pairs={{0,64},{4,68},{8,72},{12,76},{16,80},{20,84},{24,88},{28,92},{32,9... | collective-permute-start | bytes 786440 | tf_op jit(solution)/shard_map/ppermute | solution.py:12
  19.2 19.0 %collective-permute-start.5 = (bf16[32,64,128]{2,0,1:T(8,128)(2,1)S(1)}, bf16[32,64,128]{2,0,1:T(8,128)(2,1)S(1)}, u32[]{:S(2)}, u32[]{:S(2)}) collective-permute-start(bf16[32,64,128]{2,0,1:T(8,128)(2,1)S(1)} %maximum_select_fusion.2), channel_id=1, source_target_pairs={{0,128},{4,132},{8,136},{12,140},{16,144},{20,148},{24,152},{28,15... | collective-permute-start | bytes 1572872 | tf_op jit(solution)/shard_map/ppermute | solution.py:12
  22.4 4.7 %collective-permute-start = (bf16[4,64,128]{2,0,1:T(4,128)(2,1)S(1)}, bf16[4,64,128]{2,0,1:T(4,128)(2,1)S(1)}, u32[]{:S(2)}, u32[]{:S(2)}) collective-permute-start(bf16[4,64,128]{2,0,1:T(4,128)(2,1)S(1)} %copy.76), channel_id=1, source_target_pairs={{0,4},{4,0},{8,12},{12,8},{16,20},{20,16},{24,28},{28,24},{32,36},... | collective-permute-start | bytes 196616 | tf_op jit(solution)/shard_map/ppermute | solution.py:12
  27.3 9.5 %collective-permute-start.1 = (bf16[8,64,128]{2,0,1:T(8,128)(2,1)S(1)}, bf16[8,64,128]{2,0,1:T(8,128)(2,1)S(1)}, u32[]{:S(2)}, u32[]{:S(2)}) collective-permute-start(bf16[8,64,128]{2,0,1:T(8,128)(2,1)S(1)} %maximum_select_fusion.16), channel_id=1, source_target_pairs={{0,8},{4,12},{8,0},{12,4},{16,24},{20,28},{24,16},{28,20},{32,40},... | collective-permute-start | bytes 393224 | tf_op jit(solution)/shard_map/ppermute | solution.py:12
  44.9 3.9 %collective-permute-start.6 = (bf16[1,8,4,16,128]{4,3,2,1,0:T(8,128)(2,1)S(1)}, bf16[1,8,4,16,128]{4,3,2,1,0:T(8,128)(2,1)S(1)}, u32[]{:S(2)}, u32[]{:S(2)}) collective-permute-start(bf16[1,8,4,16,128]{4,3,2,1,0:T(8,128)(2,1)S(1)} %get-tuple-element.27), channel_id=1, source_target_pairs={{0,16},{4,20},{8,24},{12,28},{16,0},{20,4},{24,8},{28,12},{32,48},... | collective-permute-start | bytes 393224 | tf_op jit(solution)/shard_map/ppermute | solution.py:12
  48.9 5.4 %collective-permute-start.7 = (bf16[2,4,4,16,128]{4,3,2,1,0:T(8,128)(2,1)S(1)}, bf16[2,4,4,16,128]{4,3,2,1,0:T(8,128)(2,1)S(1)}, u32[]{:S(2)}, u32[]{:S(2)}) collective-permute-start(bf16[2,4,4,16,128]{4,3,2,1,0:T(8,128)(2,1)S(1)} %get-tuple-element.25), channel_id=1, source_target_pairs={{0,32},{4,36},{8,40},{12,44},{16,48},{20,52},{24,56},{28,60},{32,0... | collective-permute-start | bytes 393224 | tf_op jit(solution)/shard_map/ppermute | solution.py:12
  54.3 26.3 %copy-start.3 = (bf16[2,128,128]{2,1,0:T(8,128)(2,1)S(1)}, bf16[2,128,128]{2,1,0:T(8,128)(2,1)}, u32[]{:S(2)}) copy-start(bf16[2,128,128]{2,1,0:T(8,128)(2,1)} %param.6) | copy-start | bytes 196612
  54.4 3.9 %collective-permute-start.8 = (bf16[4,2,4,16,128]{4,3,2,1,0:T(8,128)(2,1)S(1)}, bf16[4,2,4,16,128]{4,3,2,1,0:T(8,128)(2,1)S(1)}, u32[]{:S(2)}, u32[]{:S(2)}) collective-permute-start(bf16[4,2,4,16,128]{4,3,2,1,0:T(8,128)(2,1)S(1)} %get-tuple-element.23), channel_id=1, source_target_pairs={{0,64},{4,68},{8,72},{12,76},{16,80},{20,84},{24,88},{28,92},{32,9... | collective-permute-start | bytes 393224 | tf_op jit(solution)/shard_map/ppermute | solution.py:12
  58.3 27.7 %copy-start = (bf16[4,64,128]{2,1,0:T(8,128)(2,1)S(1)}, bf16[4,64,128]{2,1,0:T(8,128)(2,1)}, u32[]{:S(2)}) copy-start(bf16[4,64,128]{2,1,0:T(8,128)(2,1)} %param.4) | copy-start | bytes 196612
  58.3 27.7 %copy-start.2 = (bf16[2,128,128]{2,1,0:T(8,128)(2,1)S(1)}, bf16[2,128,128]{2,1,0:T(8,128)(2,1)}, u32[]{:S(2)}) copy-start(bf16[2,128,128]{2,1,0:T(8,128)(2,1)} %param.7) | copy-start | bytes 196612
  58.3 28.4 %copy-start.1 = (bf16[2,128,512]{2,1,0:T(8,128)(2,1)S(1)}, bf16[2,128,512]{2,1,0:T(8,128)(2,1)}, u32[]{:S(2)}) copy-start(bf16[2,128,512]{2,1,0:T(8,128)(2,1)} %param.5) | copy-start | bytes 786436
  58.4 5.6 %collective-permute-start.9 = (bf16[8,1,4,16,128]{4,3,2,0,1:T(8,128)(2,1)S(1)}, bf16[8,1,4,16,128]{4,3,2,0,1:T(8,128)(2,1)S(1)}, u32[]{:S(2)}, u32[]{:S(2)}) collective-permute-start(bf16[8,1,4,16,128]{4,3,2,0,1:T(8,128)(2,1)S(1)} %get-tuple-element.21), channel_id=1, source_target_pairs={{0,128},{4,132},{8,136},{12,140},{16,144},{20,148},{24,152},{28,15... | collective-permute-start | bytes 393224 | tf_op jit(solution)/shard_map/ppermute | solution.py:12
  64.8 20.9 %all-to-all-start = ((bf16[4,4,64,128]{3,2,1,0:T(8,128)(2,1)}), bf16[4,4,64,128]{3,2,1,0:T(8,128)(2,1)S(1)}, u32[]{:S(2)}, u32[]{:S(2)}) async-start(bf16[4,4,64,128]{3,2,1,0:T(8,128)(2,1)} %copy.88), calls=%async_computation | async-start | bytes 524288 | tf_op jit(solution)/shard_map/all_to_all | solution.py:22
  119.9 3.2 %collective-permute-start.12 = (bf16[4,64,128]{2,0,1:T(4,128)(2,1)S(1)}, bf16[4,64,128]{2,0,1:T(4,128)(2,1)S(1)}, u32[]{:S(2)}, u32[]{:S(2)}) collective-permute-start(bf16[4,64,128]{2,0,1:T(4,128)(2,1)S(1)} %get-tuple-element.29), channel_id=1, source_target_pairs={{0,16},{4,20},{8,24},{12,28},{16,0},{20,4},{24,8},{28,12},{32,48},... | collective-permute-start | bytes 196616 | tf_op jit(solution)/shard_map/ppermute | solution.py:12
  123.2 5.4 %collective-permute-start.13 = (bf16[8,64,128]{2,0,1:T(8,128)(2,1)S(1)}, bf16[8,64,128]{2,0,1:T(8,128)(2,1)S(1)}, u32[]{:S(2)}, u32[]{:S(2)}) collective-permute-start(bf16[8,64,128]{2,0,1:T(8,128)(2,1)S(1)} %maximum_select_fusion.19), channel_id=1, source_target_pairs={{0,32},{4,36},{8,40},{12,44},{16,48},{20,52},{24,56},{28,60},{32,0... | collective-permute-start | bytes 393224 | tf_op jit(solution)/shard_map/ppermute | solution.py:12
  128.7 5.3 %collective-permute-start.14 = (bf16[16,64,128]{2,0,1:T(8,128)(2,1)S(1)}, bf16[16,64,128]{2,0,1:T(8,128)(2,1)S(1)}, u32[]{:S(2)}, u32[]{:S(2)}) collective-permute-start(bf16[16,64,128]{2,0,1:T(8,128)(2,1)S(1)} %maximum_select_fusion.15), channel_id=1, source_target_pairs={{0,64},{4,68},{8,72},{12,76},{16,80},{20,84},{24,88},{28,92},{32,9... | collective-permute-start | bytes 786440 | tf_op jit(solution)/shard_map/ppermute | solution.py:12
  134.2 16.7 %collective-permute-start.15 = (bf16[32,64,128]{2,0,1:T(8,128)(2,1)S(1)}, bf16[32,64,128]{2,0,1:T(8,128)(2,1)S(1)}, u32[]{:S(2)}, u32[]{:S(2)}) collective-permute-start(bf16[32,64,128]{2,0,1:T(8,128)(2,1)S(1)} %maximum_select_fusion.7), channel_id=1, source_target_pairs={{0,128},{4,132},{8,136},{12,140},{16,144},{20,148},{24,152},{28,15... | collective-permute-start | bytes 1572872 | tf_op jit(solution)/shard_map/ppermute | solution.py:12
  134.7 4.7 %collective-permute-start.10 = (bf16[4,64,128]{2,0,1:T(4,128)(2,1)S(1)}, bf16[4,64,128]{2,0,1:T(4,128)(2,1)S(1)}, u32[]{:S(2)}, u32[]{:S(2)}) collective-permute-start(bf16[4,64,128]{2,0,1:T(4,128)(2,1)S(1)} %get-tuple-element.30), channel_id=1, source_target_pairs={{0,4},{4,0},{8,12},{12,8},{16,20},{20,16},{24,28},{28,24},{32,36},... | collective-permute-start | bytes 196616 | tf_op jit(solution)/shard_map/ppermute | solution.py:12
  139.6 9.9 %collective-permute-start.11 = (bf16[8,64,128]{2,0,1:T(8,128)(2,1)S(1)}, bf16[8,64,128]{2,0,1:T(8,128)(2,1)S(1)}, u32[]{:S(2)}, u32[]{:S(2)}) collective-permute-start(bf16[8,64,128]{2,0,1:T(8,128)(2,1)S(1)} %maximum_select_fusion.18), channel_id=1, source_target_pairs={{0,8},{4,12},{8,0},{12,4},{16,24},{20,28},{24,16},{28,20},{32,40},... | collective-permute-start | bytes 393224 | tf_op jit(solution)/shard_map/ppermute | solution.py:12
  157.6 3.9 %collective-permute-start.16 = (bf16[1,8,4,16,128]{4,3,2,1,0:T(8,128)(2,1)S(1)}, bf16[1,8,4,16,128]{4,3,2,1,0:T(8,128)(2,1)S(1)}, u32[]{:S(2)}, u32[]{:S(2)}) collective-permute-start(bf16[1,8,4,16,128]{4,3,2,1,0:T(8,128)(2,1)S(1)} %get-tuple-element.19), channel_id=1, source_target_pairs={{0,16},{4,20},{8,24},{12,28},{16,0},{20,4},{24,8},{28,12},{32,48},... | collective-permute-start | bytes 393224 | tf_op jit(solution)/shard_map/ppermute | solution.py:12
  161.6 5.4 %collective-permute-start.17 = (bf16[2,4,4,16,128]{4,3,2,1,0:T(8,128)(2,1)S(1)}, bf16[2,4,4,16,128]{4,3,2,1,0:T(8,128)(2,1)S(1)}, u32[]{:S(2)}, u32[]{:S(2)}) collective-permute-start(bf16[2,4,4,16,128]{4,3,2,1,0:T(8,128)(2,1)S(1)} %get-tuple-element.17), channel_id=1, source_target_pairs={{0,32},{4,36},{8,40},{12,44},{16,48},{20,52},{24,56},{28,60},{32,0... | collective-permute-start | bytes 393224 | tf_op jit(solution)/shard_map/ppermute | solution.py:12
  167.1 4.2 %collective-permute-start.18 = (bf16[4,2,4,16,128]{4,3,2,1,0:T(8,128)(2,1)S(1)}, bf16[4,2,4,16,128]{4,3,2,1,0:T(8,128)(2,1)S(1)}, u32[]{:S(2)}, u32[]{:S(2)}) collective-permute-start(bf16[4,2,4,16,128]{4,3,2,1,0:T(8,128)(2,1)S(1)} %get-tuple-element.15), channel_id=1, source_target_pairs={{0,64},{4,68},{8,72},{12,76},{16,80},{20,84},{24,88},{28,92},{32,9... | collective-permute-start | bytes 393224 | tf_op jit(solution)/shard_map/ppermute | solution.py:12
  171.3 5.4 %collective-permute-start.19 = (bf16[8,1,4,16,128]{4,3,2,0,1:T(8,128)(2,1)S(1)}, bf16[8,1,4,16,128]{4,3,2,0,1:T(8,128)(2,1)S(1)}, u32[]{:S(2)}, u32[]{:S(2)}) collective-permute-start(bf16[8,1,4,16,128]{4,3,2,0,1:T(8,128)(2,1)S(1)} %get-tuple-element.13), channel_id=1, source_target_pairs={{0,128},{4,132},{8,136},{12,140},{16,144},{20,148},{24,152},{28,15... | collective-permute-start | bytes 393224 | tf_op jit(solution)/shard_map/ppermute | solution.py:12
  177.5 22.5 %all-to-all-start.3 = ((bf16[4,4,64,128]{3,2,1,0:T(8,128)(2,1)}), bf16[4,4,64,128]{3,2,1,0:T(8,128)(2,1)S(1)}, u32[]{:S(2)}, u32[]{:S(2)}) async-start(bf16[4,4,64,128]{3,2,1,0:T(8,128)(2,1)} %copy.96), calls=%async_computation.3 | async-start | bytes 524288 | tf_op jit(solution)/shard_map/all_to_all | solution.py:22
where the time goes:
time: 202 us; the launch traced here: 201 us
  waiting for transfers between devices  77.3 us (38%)
  starting transfers between devices  64.6 us (32%)
  blocking collectives  30.6 us (15%)
  local copies, waits for them, and re-layouts  13.4 us (7%)
  other arithmetic  7.54 us (4%)
  matrix products  7.34 us (4%)
    ppermute x20, waiting for transfers between devices, swapped(): return lax.ppermute(value, axis, pairs)  67.6 us
    all_to_all x2, starting transfers between devices, sum_at_owner(): tiles = lax.all_to_all(in_blocks(x, dim, size), axis, 0, 0, tiled=True)  33.3 us
    ppermute x20, starting transfers between devices, swapped(): return lax.ppermute(value, axis, pairs)  31.3 us
    all_to_all x2, blocking collectives, side_by_side(): lax.all_to_all(both, axis, split_axis=split_dim, concat_axis=concat_dim,...  30.6 us
    all_to_all x2, waiting for transfers between devices, sum_at_owner(): tiles = lax.all_to_all(in_blocks(x, dim, size), axis, 0, 0, tiled=True)  9.72 us
    select_n x4, local copies, waits for them, and re-layouts, doubling(): jnp.where(upper, jnp.concatenate([other, values], 0), jnp.concatenate([va...  9.59 us
    dot_general x2, matrix products, blocked_partial(): jnp.einsum('ikh,jkh->ijh', left_all, right_all, preferred_element_type=jn...  4.44 us
  transfers between devices with their start and end apart: 22, of which 20 were waited for; matrix products, arithmetic and copies ran while one was open for 2% of the time, Pallas kernels for 0%

commit v1 on v0

v1 whole, which is shorter than its diff:
```python
import jax
import jax.numpy as jnp
from jax import lax
from jax.experimental import pallas as pl
from jax.experimental.pallas import tpu as pltpu
from jax.sharding import Mesh, PartitionSpec as P

EPSILON = 1e-05
BF16 = jnp.bfloat16
F32 = jnp.float32

CHIPS = ("zl", "y", "x", "zh")


def nn(a, b):
    return lax.dot_general(a, b, (((1,), (0,)), ((), ())), preferred_element_type=F32)


def nt(a, b):
    return lax.dot_general(a, b, (((1,), (1,)), ((), ())), preferred_element_type=F32)


def picks(rows, cols, source):
    row = lax.broadcasted_iota(jnp.int32, (rows, cols), 0)
    col = lax.broadcasted_iota(jnp.int32, (rows, cols), 1)
    return (col == source(row)).astype(F32).astype(BF16)


def moved(one_hot, values):
    return nn(one_hot, values).astype(BF16)


def interleaved(parts, per_block):
    count = len(parts)
    size = count * per_block
    shuffle = picks(size, size, lambda i: i % count * per_block + i // count)
    blocks = []
    for start in range(0, parts[0].shape[0], per_block):
        stacked = jnp.concatenate([p[start : start + per_block] for p in parts], 0)
        blocks.append(moved(shuffle, stacked))
    return jnp.concatenate(blocks, 0)


def normalized(values):
    shifted = values - jnp.mean(values, axis=0, keepdims=True)
    spread = jnp.mean(shifted * shifted, axis=0, keepdims=True)
    return (shifted * lax.rsqrt(spread + EPSILON)).astype(BF16)


def sigmoid(x):
    return 1.0 / (1.0 + jnp.exp(-x))


def operands(weights, normed):
    projected = nn(weights, normed)
    left = sigmoid(projected[0:128]) * projected[128:256]
    right = sigmoid(projected[256:384]) * projected[384:512]
    return left.astype(BF16), right.astype(BF16)


def halves_swapped(a, b):
    low = lax.broadcasted_iota(jnp.int32, a.shape, 1) < 64
    rolled_a, rolled_b = jnp.roll(a, 64, 1), jnp.roll(b, 64, 1)
    return jnp.where(low, a, rolled_b), jnp.where(low, rolled_a, b)


def identity(size):
    return picks(size, size, lambda i: i)


def first_math(core, own, partner, in_w, gate_w):
    own_t = nt(identity(128), own)
    partner_t = nt(identity(128), partner)
    gate = sigmoid(nn(gate_w, normalized(own_t)))
    pieces = []
    for pair in range(2):
        mine = own_t[:, 128 * pair : 128 * pair + 128]
        other = partner_t[:, 128 * pair : 128 * pair + 128]
        lo = jnp.where(core == 0, mine, other)
        hi = jnp.where(core == 0, other, mine)
        pieces.extend(halves_swapped(lo, hi))
    both = jnp.concatenate(pieces, 1)
    left, right = operands(in_w, normalized(both))
    parts = [v[:, 128 * r : 128 * r + 128] for v in (left, right) for r in range(4)]
    return interleaved(parts, 32), own_t, gate


def returned(total_even, total_odd):
    out = halves_swapped(total_even, total_odd)
    return jnp.concatenate(out, 0).astype(BF16)


def outgoing_math(core, received):
    take_left = picks(256, 512, lambda i: i % 128 // 2 * 8 + i % 2 * 2 + i // 128)
    take_right = picks(
        128, 512, lambda j: (j // 64 * 32 + core * 16 + j % 64 // 4) * 8 + 4 + j % 4
    )
    total = 0.0
    for zl in range(2):
        block = received[512 * zl : 512 * zl + 512]
        total += nt(moved(take_left, block), moved(take_right, block))
    return returned(total[0:128], total[128:256])


def residual(gathered, out_w, state, gate):
    split = nn(picks(256, 256, lambda i: i % 128 * 2 + i // 128), gathered)
    product = jnp.concatenate([split[0:128], split[128:256]], 1)
    return (state + gate * nn(out_w, normalized(product))).astype(BF16)


def middle_math(gathered, state, gate, out_w, in_w, gate_w):
    middle = residual(gathered, out_w, state, gate).astype(F32)
    normed = normalized(middle)
    left, right = operands(in_w, normed)
    next_gate = sigmoid(nn(gate_w, normed))
    parts = [v[:, 128 * r : 128 * r + 128] for v in (left, right) for r in range(2)]
    return interleaved(parts, 64), middle, next_gate


def incoming_math(core, received, partner_left):
    take_left = picks(128, 256, lambda i: i // 2 * 4 + i % 2)
    take_right = picks(128, 256, lambda i: i // 2 * 4 + 2 + i % 2)
    lanes = picks(128, 128, lambda i: i // 64 * 64 + i % 32 * 2 + i % 64 // 32)
    lefts, rights = {}, []
    for zl in range(2):
        block = received[256 * zl : 256 * zl + 256]
        mine = nt(lanes, moved(take_left, block)).astype(BF16)
        other = nt(lanes, partner_left[128 * zl : 128 * zl + 128]).astype(BF16)
        lefts[zl, 0] = jnp.where(core == 0, mine, other)
        lefts[zl, 1] = jnp.where(core == 0, other, mine)
        rights.append(nn(take_right, block))
    right = jnp.concatenate(halves_swapped(*rights), 0).astype(BF16)
    order = [lefts[zl, c] for zl in range(2) for c in range(2)]
    totals = []
    for odd in range(2):
        rows = [
            jnp.concatenate([v[32 * odd : 32 * odd + 32], v[64 + 32 * odd : 96 + 32 * odd]], 1)
            for v in order
        ]
        totals.append(nn(jnp.concatenate(rows, 0), right))
    return returned(*totals)


def last_math(gathered, state, gate, out_w):
    refined = residual(gathered, out_w, state, gate)
    return nt(identity(256), refined).astype(BF16)


def first_kernel(core, own, partner, in_w, gate_w, sent, state, gate):
    sent[...], state[...], gate[...] = first_math(
        core[0], own[...], partner[...], in_w[...], gate_w[...]
    )


def outgoing_kernel(core, received, sent):
    sent[...] = outgoing_math(core[0], received[...])


def middle_kernel(gathered, state, gate, out_w, in_w, gate_w, sent, middle, next_gate):
    sent[...], middle[...], next_gate[...] = middle_math(
        gathered[...], state[...], gate[...], out_w[...], in_w[...], gate_w[...]
    )


def incoming_kernel(core, received, partner_left, sent):
    sent[...] = incoming_math(core[0], received[...], partner_left[...])


def last_kernel(gathered, state, gate, out_w, refined):
    refined[...] = last_math(gathered[...], state[...], gate[...], out_w[...])


def call(kernel, outs, scalars, *arrays):
    smem = pl.BlockSpec(memory_space=pltpu.SMEM)
    vmem = pl.BlockSpec(memory_space=pltpu.VMEM)
    shapes = tuple(jax.ShapeDtypeStruct(shape, dtype) for shape, dtype in outs)
    return pl.pallas_call(
        kernel,
        out_shape=shapes,
        in_specs=[smem] * len(scalars) + [vmem] * len(arrays),
        out_specs=tuple(vmem for _ in shapes),
    )(*scalars, *arrays)


def exchanged(rows, per_chip):
    blocks = rows.reshape(128, per_chip, 128)
    return lax.all_to_all(blocks, CHIPS, 0, 0, tiled=True)


def from_partner(value):
    return lax.ppermute(value, "c", [(0, 1), (1, 0)])


def per_device(pair_rep, in_weights, gate_weights, out_weights):
    core = lax.axis_index("c").astype(jnp.int32).reshape(1)
    own = pair_rep.reshape(256, 128)
    partner = from_partner(own)
    in_w = jnp.swapaxes(in_weights, 1, 2)
    gate_w = jnp.swapaxes(gate_weights, 1, 2)
    out_w = jnp.swapaxes(out_weights, 1, 2)
    state_like = ((128, 256), F32)
    sent, state, gate = call(
        first_kernel, [((1024, 128), BF16), state_like, state_like], (core,),
        own, partner, in_w[0], gate_w[0],
    )
    received = exchanged(sent, 8).reshape(1024, 128)
    (sent,) = call(outgoing_kernel, [((256, 128), BF16)], (core,), received)
    gathered = exchanged(sent, 2).reshape(256, 128)
    sent, middle, gate = call(
        middle_kernel, [((512, 128), BF16), state_like, state_like], (),
        gathered, state, gate, out_w[0], in_w[1], gate_w[1],
    )
    received = exchanged(sent, 4)
    partner_left = from_partner(received[:, 0:2]).reshape(256, 128)
    (sent,) = call(
        incoming_kernel, [((256, 128), BF16)], (core,), received.reshape(512, 128), partner_left
    )
    gathered = exchanged(sent, 2).reshape(256, 128)
    (refined,) = call(last_kernel, [((256, 128), BF16)], (), gathered, middle, gate, out_w[1])
    return refined.reshape(pair_rep.shape)


def solution(mesh):
    fine = Mesh(mesh.devices.reshape(4, 4, 4, 2, 2), ("y", "x", "zh", "zl", "c"))
    placed = P(("y", "x", "zh"), ("zl", "c"), None)
    return jax.shard_map(
        per_device, mesh=fine, in_specs=(placed, P(), P(), P()), out_specs=placed, check_vma=False
    )
```

time: 202 us -> 104 us (0.51)
  waiting for transfers between devices: 77.3 us -> 23.2 us
  starting transfers between devices: 64.6 us -> 28.2 us
  Pallas kernels: 0 us -> 12 us
  other arithmetic: 7.54 us -> 0 us
  matrix products: 7.34 us -> 0 us
  local copies, waits for them, and re-layouts: 13.4 us -> 6.08 us
  blocking collectives: 30.6 us -> 34.1 us
    ppermute x20 -> x2, waiting for transfers between devices: 67.6 us -> 0.9 us  [from_partner(): return lax.ppermute(value, 'c', [(0, 1), (1, 0)])]
    ppermute x20 -> x2, starting transfers between devices: 31.3 us -> 7.11 us  [from_partner(): return lax.ppermute(value, 'c', [(0, 1), (1, 0)])]
    all_to_all x2, waiting for transfers between devices: 9.72 us -> 22.3 us  [exchanged(): return lax.all_to_all(blocks, CHIPS, 0, 0, tiled=True)]
    all_to_all x2, starting transfers between devices: 33.3 us -> 21.1 us  [exchanged(): return lax.all_to_all(blocks, CHIPS, 0, 0, tiled=True)]
    pallas_call x0 -> x5, Pallas kernels: none -> 12 us  [call(): pl.pallas_call(kernel, out_shape=shapes, in_specs=[smem] * len(scalars) +...]
    select_n x4 -> x0, local copies, waits for them, and re-layouts: 9.59 us -> none  [doubling(): jnp.where(upper, jnp.concatenate([other, values], 0), jnp.concatenate([va...]
    dot_general x8 -> x0, matrix products: 7.34 us -> none  [the longest x2 4.44 us: blocked_partial(): jnp.einsum('ikh,jkh->ijh', left_all, right_all, preferred_element_type=jn...]
    unnamed x10 -> x17, local copies, waits for them, and re-layouts: 0.21 us -> 4.05 us
  transfers between devices with their start and end apart: 22 -> 4, of which waited for: 20 -> 3; matrix products, arithmetic and copies ran while one was open for 2% -> 3% of each run, Pallas kernels for 0% -> 0%
where the time goes in v1:
time: 104 us
  blocking collectives  34.1 us (33%)
  starting transfers between devices  28.2 us (27%)
  waiting for transfers between devices  23.2 us (22%)
  Pallas kernels  12 us (12%)
  local copies, waits for them, and re-layouts  6.08 us (6%)
    all_to_all x2, blocking collectives, exchanged(): return lax.all_to_all(blocks, CHIPS, 0, 0, tiled=True)  34.1 us
    all_to_all x2, waiting for transfers between devices, exchanged(): return lax.all_to_all(blocks, CHIPS, 0, 0, tiled=True)  22.3 us
    all_to_all x2, starting transfers between devices, exchanged(): return lax.all_to_all(blocks, CHIPS, 0, 0, tiled=True)  21.1 us
    pallas_call x5, Pallas kernels, call(): pl.pallas_call(kernel, out_shape=shapes, in_specs=[smem] * len(scalars) +...  12 us
    ppermute x2, starting transfers between devices, from_partner(): return lax.ppermute(value, 'c', [(0, 1), (1, 0)])  7.11 us
    unnamed x17, local copies, waits for them, and re-layouts  4.05 us
  transfers between devices with their start and end apart: 4, of which 3 were waited for; matrix products, arithmetic and copies ran while one was open for 3% of the time, Pallas kernels for 0%

profile of v1, /device:TPU:1, one launch (start us, length us, event | category | flops | bytes accessed | tf_op | source)
XLA Modules:
  0.0 103.7 jit_solution(4579012766026888121)
XLA Ops:
  0.0 3.2 %collective-permute-start = (bf16[256,128]{1,0:T(8,128)(2,1)}, bf16[256,128]{1,0:T(8,128)(2,1)S(1)}, u32[]{:S(2)}, u32[]{:S(2)}) collective-permute-start(bf16[256,128]{1,0:T(8,128)(2,1)} %bitcast.38), channel_id=1, source_target_pairs={{0,1},{1,0},{2,3},{3,2},{4,5},{5,4},{6,7},{7,6},{8,9},{9,8},{10,11... | collective-permute-start | bytes 196616 | tf_op jit(solution)/shard_map/ppermute | solution.py:191
  3.2 1.1 %copy.5 = bf16[2,128,512]{1,2,0:T(8,128)(2,1)S(1)} copy(bf16[2,128,512]{2,1,0:T(8,128)(2,1)} %param.5) | data formatting | bytes 524288 | tf_op args[1]
  4.3 0.0 copy-start.3
  4.3 0.7 slice_bitcast_fusion
  5.1 0.1 copy-done.3
  5.2 0.1 copy.6
  5.3 0.6 slice_bitcast_fusion.3
  5.9 0.0 collective-permute-done.partner
  5.9 0.0 copy-start.5
  5.9 0.6 copy-done.5
  6.6 2.6 %shard_map.46 = (bf16[1024,128]{1,0:T(8,128)(2,1)}, f32[128,256]{1,0:T(8,128)}, f32[128,256]{1,0:T(8,128)}) custom-call(s32[1]{0:T(128)} %bitcast.core, bf16[256,128]{1,0:T(8,128)(2,1)} %bitcast.39, bf16[256,128]{1,0:T(8,128)(2,1)} %copy-done.5, bf16[512,128]{1,0:T(8,128)(2,1)} %get-tuple-element.18.in_w, bf16[128,128]{1,0:T(8,128)(2,1)} %get-tuple-element.22.gate_w), custom_call_target="tpu_custom_call" | custom-call | tf_op jit(solution)/shard_map/pallas_call | solution.py:177
  9.1 0.0 copy-start.4
  9.1 13.9 %all-to-all-start = ((bf16[128,8,128]{2,1,0:T(8,128)(2,1)}), bf16[128,8,128]{2,1,0:T(8,128)(2,1)S(1)}, u32[]{:S(2)}, u32[]{:S(2)}) async-start(bf16[128,8,128]{2,1,0:T(8,128)(2,1)} %bitcast.31), calls=%async_computation | async-start | bytes 524288 | tf_op jit(solution)/shard_map/all_to_all | solution.py:187
  23.1 0.0 copy-done.4
  23.1 0.1 copy.7
  23.2 13.0 %all-to-all-done = bf16[128,8,128]{2,1,0:T(8,128)(2,1)S(1)} async-done(((bf16[128,8,128]{2,1,0:T(8,128)(2,1)}), bf16[128,8,128]{2,1,0:T(8,128)(2,1)S(1)}, u32[]{:S(2)}, u32[]{:S(2)}) %all-to-all-start) | async-done | bytes 262176 | tf_op jit(solution)/shard_map/all_to_all | solution.py:187
  36.2 0.0 copy-start
  36.2 0.7 copy-done
  36.9 2.3 %shard_map.47 = bf16[256,128]{1,0:T(8,128)(2,1)} custom-call(s32[1]{0:T(128)} %bitcast.core, bf16[1024,128]{1,0:T(8,128)(2,1)} %bitcast.27), custom_call_target="tpu_custom_call" | custom-call | tf_op jit(solution)/shard_map/pallas_call | solution.py:177
  39.1 7.2 %all-to-all-start.1 = ((bf16[128,2,128]{2,1,0:T(2,128)(2,1)}), bf16[128,2,128]{2,1,0:T(2,128)(2,1)S(1)}, u32[]{:S(2)}, u32[]{:S(2)}) async-start(bf16[128,2,128]{2,1,0:T(2,128)(2,1)} %bitcast.30), calls=%async_computation.1 | async-start | bytes 131072 | tf_op jit(solution)/shard_map/all_to_all | solution.py:187
  46.3 0.6 slice_bitcast_fusion.2
  47.0 9.4 %all-to-all-done.1 = bf16[128,2,128]{2,1,0:T(2,128)(2,1)S(1)} async-done(((bf16[128,2,128]{2,1,0:T(2,128)(2,1)}), bf16[128,2,128]{2,1,0:T(2,128)(2,1)S(1)}, u32[]{:S(2)}, u32[]{:S(2)}) %all-to-all-start.1) | async-done | bytes 65568 | tf_op jit(solution)/shard_map/all_to_all | solution.py:187
  56.3 0.0 copy-start.2
  56.3 0.6 copy-done.2
  57.0 2.7 %shard_map.48 = (bf16[512,128]{1,0:T(8,128)(2,1)}, f32[128,256]{1,0:T(8,128)}, f32[128,256]{1,0:T(8,128)}) custom-call(bf16[256,128]{1,0:T(8,128)(2,1)} %bitcast.36, f32[128,256]{1,0:T(8,128)} %get-tuple-element.12.state, f32[128,256]{1,0:T(8,128)} %get-tuple-element.13.gate, bf16[128,128]{1,0:T(8,128)(2,1)} %get-tuple-element.20.out_w, ...), custom_call_target="tpu_custom_call" | custom-call | tf_op jit(solution)/shard_map/pallas_call | solution.py:177
  59.6 16.6 %all_to_all.20 = bf16[128,4,128]{2,1,0:T(4,128)(2,1)S(1)} all-to-all(bf16[128,4,128]{2,1,0:T(4,128)(2,1)} %bitcast.37), channel_id=1, replica_groups=mesh['y'=4,'x'=4,'zh'=4,'zl'=2,'c'=2] {'zl','y','x','zh'}, dimensions={0} | all-to-all | bytes 262144 | tf_op jit(solution)/shard_map/all_to_all | solution.py:187
  76.3 0.0 copy-start.1
  76.3 3.9 %collective-permute-start.1 = (bf16[128,2,128]{2,1,0:T(2,128)(2,1)S(1)}, bf16[128,2,128]{2,1,0:T(2,128)(2,1)S(1)}, u32[]{:S(2)}, u32[]{:S(2)}) collective-permute-start(bf16[128,2,128]{2,1,0:T(2,128)(2,1)S(1)} %slice.33), channel_id=1, source_target_pairs={{0,1},{1,0},{2,3},{3,2},{4,5},{5,4},{6,7},{7,6},{8,9},{9,8},{10,11... | collective-permute-start | bytes 196616 | tf_op jit(solution)/shard_map/ppermute | solution.py:191
  80.3 0.9 collective-permute-done.1
  81.2 0.0 copy-start.6
  81.2 0.0 copy-done.1
  81.2 0.6 copy-done.6
  81.8 2.2 %shard_map.49 = bf16[256,128]{1,0:T(8,128)(2,1)} custom-call(s32[1]{0:T(128)} %bitcast.core, bf16[512,128]{1,0:T(8,128)(2,1)} %bitcast.29, bf16[256,128]{1,0:T(8,128)(2,1)} %bitcast.40), custom_call_target="tpu_custom_call" | custom-call | tf_op jit(solution)/shard_map/pallas_call | solution.py:177
  84.0 17.4 %all_to_all.21 = bf16[128,2,128]{2,1,0:T(2,128)(2,1)} all-to-all(bf16[128,2,128]{2,1,0:T(2,128)(2,1)} %bitcast.35), channel_id=1, replica_groups=mesh['y'=4,'x'=4,'zh'=4,'zl'=2,'c'=2] {'zl','y','x','zh'}, dimensions={0} | all-to-all | bytes 131072 | tf_op jit(solution)/shard_map/all_to_all | solution.py:187
  101.5 2.2 %shard_map.50 = bf16[256,128]{1,0:T(8,128)(2,1)} custom-call(bf16[256,128]{1,0:T(8,128)(2,1)} %bitcast.34, f32[128,256]{1,0:T(8,128)} %get-tuple-element.15.state, f32[128,256]{1,0:T(8,128)} %get-tuple-element.16.gate, bf16[128,128]{1,0:T(8,128)(2,1)} %get-tuple-element.19.out_w), custom_call_target="tpu_custom_call" | custom-call | tf_op jit(solution)/shard_map/pallas_call | solution.py:177
  (1 shorter events, 0.0 us)
Async XLA Ops:
  0.0 5.9 %collective-permute-start = (bf16[256,128]{1,0:T(8,128)(2,1)}, bf16[256,128]{1,0:T(8,128)(2,1)S(1)}, u32[]{:S(2)}, u32[]{:S(2)}) collective-permute-start(bf16[256,128]{1,0:T(8,128)(2,1)} %bitcast.38), channel_id=1, source_target_pairs={{0,1},{1,0},{2,3},{3,2},{4,5},{5,4},{6,7},{7,6},{8,9},{9,8},{10,11... | collective-permute-start | bytes 196616 | tf_op jit(solution)/shard_map/ppermute | solution.py:191
  4.3 0.8 copy-start.3
  5.9 0.6 copy-start.5
  9.1 13.9 %copy-start.4 = (bf16[2,128,128]{2,1,0:T(8,128)(2,1)S(1)}, bf16[2,128,128]{2,1,0:T(8,128)(2,1)}, u32[]{:S(2)}) copy-start(bf16[2,128,128]{2,1,0:T(8,128)(2,1)} %param.7) | copy-start | bytes 196612
  9.1 27.0 %all-to-all-start = ((bf16[128,8,128]{2,1,0:T(8,128)(2,1)}), bf16[128,8,128]{2,1,0:T(8,128)(2,1)S(1)}, u32[]{:S(2)}, u32[]{:S(2)}) async-start(bf16[128,8,128]{2,1,0:T(8,128)(2,1)} %bitcast.31), calls=%async_computation | async-start | bytes 524288 | tf_op jit(solution)/shard_map/all_to_all | solution.py:187
  36.2 0.7 copy-start
  39.1 17.2 %all-to-all-start.1 = ((bf16[128,2,128]{2,1,0:T(2,128)(2,1)}), bf16[128,2,128]{2,1,0:T(2,128)(2,1)S(1)}, u32[]{:S(2)}, u32[]{:S(2)}) async-start(bf16[128,2,128]{2,1,0:T(2,128)(2,1)} %bitcast.30), calls=%async_computation.1 | async-start | bytes 131072 | tf_op jit(solution)/shard_map/all_to_all | solution.py:187
  56.3 0.6 copy-start.2
  76.3 4.9 %copy-start.1 = (bf16[128,4,128]{2,1,0:T(4,128)(2,1)}, bf16[128,4,128]{2,1,0:T(4,128)(2,1)S(1)}, u32[]{:S(2)}) copy-start(bf16[128,4,128]{2,1,0:T(4,128)(2,1)S(1)} %all_to_all.20) | copy-start | bytes 393220
  76.3 4.8 %collective-permute-start.1 = (bf16[128,2,128]{2,1,0:T(2,128)(2,1)S(1)}, bf16[128,2,128]{2,1,0:T(2,128)(2,1)S(1)}, u32[]{:S(2)}, u32[]{:S(2)}) collective-permute-start(bf16[128,2,128]{2,1,0:T(2,128)(2,1)S(1)} %slice.33), channel_id=1, source_target_pairs={{0,1},{1,0},{2,3},{3,2},{4,5},{5,4},{6,7},{7,6},{8,9},{9,8},{10,11... | collective-permute-start | bytes 196616 | tf_op jit(solution)/shard_map/ppermute | solution.py:191
  81.2 0.6 copy-start.6

commit v2 on v1

v2 whole, which is shorter than its diff:
```python
import jax
import jax.numpy as jnp
from jax import lax
from jax.experimental import pallas as pl
from jax.experimental.pallas import tpu as pltpu
from jax.sharding import Mesh, PartitionSpec as P

EPSILON = 1e-05
BF16 = jnp.bfloat16
F32 = jnp.float32

CHIPS = ("zl", "y", "x", "zh")


def nn(a, b):
    return lax.dot_general(a, b, (((1,), (0,)), ((), ())), preferred_element_type=F32)


def nt(a, b):
    return lax.dot_general(a, b, (((1,), (1,)), ((), ())), preferred_element_type=F32)


def picks(rows, cols, source):
    row = lax.broadcasted_iota(jnp.int32, (rows, cols), 0)
    col = lax.broadcasted_iota(jnp.int32, (rows, cols), 1)
    return (col == source(row)).astype(F32).astype(BF16)


def moved(one_hot, values):
    return nn(one_hot, values).astype(BF16)


def interleaved(parts, per_block):
    count = len(parts)
    size = count * per_block
    shuffle = picks(size, size, lambda i: i % count * per_block + i // count)
    blocks = []
    for start in range(0, parts[0].shape[0], per_block):
        stacked = jnp.concatenate([p[start : start + per_block] for p in parts], 0)
        blocks.append(moved(shuffle, stacked))
    return jnp.concatenate(blocks, 0)


def normalized(values):
    shifted = values - jnp.mean(values, axis=0, keepdims=True)
    spread = jnp.mean(shifted * shifted, axis=0, keepdims=True)
    return (shifted * lax.rsqrt(spread + EPSILON)).astype(BF16)


def sigmoid(x):
    return 1.0 / (1.0 + jnp.exp(-x))


def operands(weights, normed):
    projected = nn(weights, normed)
    left = sigmoid(projected[0:128]) * projected[128:256]
    right = sigmoid(projected[256:384]) * projected[384:512]
    return left.astype(BF16), right.astype(BF16)


def halves_swapped(a, b):
    low = lax.broadcasted_iota(jnp.int32, a.shape, 1) < 64
    rolled_a, rolled_b = jnp.roll(a, 64, 1), jnp.roll(b, 64, 1)
    return jnp.where(low, a, rolled_b), jnp.where(low, rolled_a, b)


def identity(size):
    return picks(size, size, lambda i: i)


def transposed(weights):
    eye = identity(128)
    blocks = [nt(eye, weights[:, k : k + 128]) for k in range(0, weights.shape[1], 128)]
    return jnp.concatenate(blocks, 0).astype(BF16)


def sent_operands(weights, normed):
    left, right = operands(transposed(weights), normed)
    parts = [v[:, 128 * r : 128 * r + 128] for v in (left, right) for r in range(2)]
    return interleaved(parts, 64)


def first_math(own, in_w, gate_w):
    state = nt(identity(128), own)
    normed = normalized(state)
    return sent_operands(in_w, normed), state, sigmoid(nn(transposed(gate_w), normed))


def by_core(core, mine, other):
    return jnp.where(core == 0, mine, other), jnp.where(core == 0, other, mine)


def returned(total_even, total_odd):
    out = halves_swapped(total_even, total_odd)
    return jnp.concatenate(out, 0).astype(BF16)


def outgoing_math(core, received, partner):
    take_left = picks(128, 256, lambda i: i // 2 * 4 + i % 2)
    take_right = picks(64, 256, lambda j: (j // 32 * 32 + core * 16 + j % 32 // 2) * 4 + 2 + j % 2)
    ordered = picks(128, 128, lambda j: j % 2 * 64 + j // 2)
    lefts, rights = ([], []), ([], [])
    for zl in range(2):
        mine = received[256 * zl : 256 * zl + 256]
        other = partner[256 * zl : 256 * zl + 256]
        for take, rows in ((take_left, lefts), (take_right, rights)):
            pair = by_core(core, nn(take, mine), nn(take, other))
            for r, half in enumerate(halves_swapped(*pair)):
                rows[r].append(half.astype(BF16))
    right = jnp.concatenate([jnp.concatenate(v, 1) for v in rights], 0)
    right = moved(ordered, right)
    return returned(*(nt(jnp.concatenate(v, 1), right) for v in lefts))


def residual(gathered, out_w, state, gate):
    split = nn(picks(256, 256, lambda i: i % 128 * 2 + i // 128), gathered)
    product = jnp.concatenate([split[0:128], split[128:256]], 1)
    update = nn(transposed(out_w), normalized(product))
    return (state + gate * update).astype(BF16)


def middle_math(gathered, state, gate, out_w, in_w, gate_w):
    middle = residual(gathered, out_w, state, gate).astype(F32)
    normed = normalized(middle)
    return sent_operands(in_w, normed), middle, sigmoid(nn(transposed(gate_w), normed))


def incoming_math(core, received, partner):
    take_left = picks(128, 256, lambda i: i // 2 * 4 + i % 2)
    take_right = picks(128, 256, lambda i: i // 2 * 4 + 2 + i % 2)
    lanes = picks(128, 128, lambda i: i // 64 * 64 + i % 32 * 2 + i % 64 // 32)
    lefts, rights = {}, []
    for zl in range(2):
        block = received[256 * zl : 256 * zl + 256]
        mine = nt(lanes, moved(take_left, block)).astype(BF16)
        there = moved(take_left, partner[256 * zl : 256 * zl + 256])
        other = nt(lanes, there).astype(BF16)
        lefts[zl, 0], lefts[zl, 1] = by_core(core, mine, other)
        rights.append(nn(take_right, block))
    right = jnp.concatenate(halves_swapped(*rights), 0).astype(BF16)
    order = [lefts[zl, c] for zl in range(2) for c in range(2)]
    totals = []
    for odd in range(2):
        rows = [
            jnp.concatenate([v[32 * odd : 32 * odd + 32], v[64 + 32 * odd : 96 + 32 * odd]], 1)
            for v in order
        ]
        totals.append(nn(jnp.concatenate(rows, 0), right))
    return returned(*totals)


def last_math(gathered, state, gate, out_w):
    refined = residual(gathered, out_w, state, gate)
    return nt(identity(256), refined).astype(BF16)


def first_kernel(own, in_w, gate_w, sent, state, gate):
    sent[...], state[...], gate[...] = first_math(own[...], in_w[0], gate_w[0])


def outgoing_kernel(received, partner, sent):
    sent[...] = outgoing_math(lax.axis_index("c"), received[...], partner[...])


def middle_kernel(gathered, state, gate, out_w, in_w, gate_w, sent, middle, next_gate):
    sent[...], middle[...], next_gate[...] = middle_math(
        gathered[...], state[...], gate[...], out_w[0], in_w[1], gate_w[1]
    )


def incoming_kernel(received, partner, sent):
    sent[...] = incoming_math(lax.axis_index("c"), received[...], partner[...])


def last_kernel(gathered, state, gate, out_w, refined):
    refined[...] = last_math(gathered[...], state[...], gate[...], out_w[1])


def call(kernel, outs, *arrays):
    vmem = pl.BlockSpec(memory_space=pltpu.VMEM)
    return pl.pallas_call(
        kernel,
        out_shape=tuple(jax.ShapeDtypeStruct(shape, dtype) for shape, dtype in outs),
        in_specs=[vmem] * len(arrays),
        out_specs=tuple(vmem for _ in outs),
        compiler_params=pltpu.CompilerParams(vmem_limit_bytes=16 << 20),
    )(*arrays)


def exchanged(rows):
    blocks = rows.reshape(128, -1, 128)
    return lax.all_to_all(blocks, CHIPS, 0, 0, tiled=True).reshape(rows.shape)


def from_partner(value):
    return lax.ppermute(value, "c", [(0, 1), (1, 0)])


def per_device(pair_rep, in_weights, gate_weights, out_weights):
    own = pair_rep.reshape(256, 128)
    operands_out, results_out = ((512, 128), BF16), ((256, 128), BF16)
    kept = ((128, 256), F32)
    sent, state, gate = call(
        first_kernel, [operands_out, kept, kept], own, in_weights, gate_weights
    )
    received = exchanged(sent)
    (sent,) = call(outgoing_kernel, [results_out], received, from_partner(received))
    sent, state, gate = call(
        middle_kernel, [operands_out, kept, kept],
        exchanged(sent), state, gate, out_weights, in_weights, gate_weights,
    )
    received = exchanged(sent)
    (sent,) = call(incoming_kernel, [results_out], received, from_partner(received))
    (refined,) = call(last_kernel, [results_out], exchanged(sent), state, gate, out_weights)
    return refined.reshape(pair_rep.shape)


def solution(mesh):
    fine = Mesh(mesh.devices.reshape(4, 4, 4, 2, 2), ("y", "x", "zh", "zl", "c"))
    placed = P(("y", "x", "zh"), ("zl", "c"), None)
    return jax.shard_map(
        per_device, mesh=fine, in_specs=(placed, P(), P(), P()), out_specs=placed, check_vma=False
    )
```

time: 104 us -> 89.7 us (0.86)
  blocking collectives: 34.1 us -> 74.8 us
  starting transfers between devices: 28.2 us -> 5.42 us
  waiting for transfers between devices: 23.2 us -> 1.97 us
  Pallas kernels: 12 us -> 4.48 us
  local copies, waits for them, and re-layouts: 6.08 us -> 2.64 us
    all_to_all x2 -> x4, blocking collectives: 34.1 us -> 74.8 us  [exchanged(): return lax.all_to_all(blocks, CHIPS, 0, 0, tiled=True).reshape(rows.shape)]
    all_to_all x2 -> x0, waiting for transfers between devices: 22.3 us -> none  [exchanged(): return lax.all_to_all(blocks, CHIPS, 0, 0, tiled=True)]
    all_to_all x2 -> x0, starting transfers between devices: 21.1 us -> none  [exchanged(): return lax.all_to_all(blocks, CHIPS, 0, 0, tiled=True)]
    pallas_call x5, Pallas kernels: 12 us -> 4.48 us  [call(): pl.pallas_call(kernel, out_shape=tuple((jax.ShapeDtypeStruct(shape, dtype...]
    squeeze x3 -> x0, local copies, waits for them, and re-layouts: 1.98 us -> none  [the longest x1 0.72 us: per_device(): in_w[1]]
    ppermute x2, starting transfers between devices: 7.11 us -> 5.42 us  [from_partner(): return lax.ppermute(value, 'c', [(0, 1), (1, 0)])]
    unnamed x17 -> x12, local copies, waits for them, and re-layouts: 4.05 us -> 2.64 us
    ppermute x2, waiting for transfers between devices: 0.9 us -> 1.97 us  [from_partner(): return lax.ppermute(value, 'c', [(0, 1), (1, 0)])]
  transfers between devices with their start and end apart: 4 -> 2, of which waited for: 3 -> 2; matrix products, arithmetic and copies ran while one was open for 3% -> 0% of each run, Pallas kernels for 0% -> 0%
where the time goes in v2:
time: 89.7 us; the launch traced here: 89.4 us
  blocking collectives  74.8 us (83%)
  starting transfers between devices  5.42 us (6%)
  Pallas kernels  4.48 us (5%)
  local copies, waits for them, and re-layouts  2.64 us (3%)
  waiting for transfers between devices  1.97 us (2%)
    all_to_all x4, blocking collectives, exchanged(): return lax.all_to_all(blocks, CHIPS, 0, 0, tiled=True).reshape(rows.shape)  74.8 us
    ppermute x2, starting transfers between devices, from_partner(): return lax.ppermute(value, 'c', [(0, 1), (1, 0)])  5.42 us
    pallas_call x5, Pallas kernels, call(): pl.pallas_call(kernel, out_shape=tuple((jax.ShapeDtypeStruct(shape, dtype...  4.48 us
    unnamed x12, local copies, waits for them, and re-layouts  2.64 us
    ppermute x2, waiting for transfers between devices, from_partner(): return lax.ppermute(value, 'c', [(0, 1), (1, 0)])  1.97 us
  transfers between devices with their start and end apart: 2, of which 2 were waited for; matrix products, arithmetic and copies ran while one was open for 0% of the time, Pallas kernels for 0%

profile of v2, /device:TPU:1, one launch (start us, length us, event | category | flops | bytes accessed | tf_op | source)
XLA Modules:
  0.0 89.4 jit_solution(16583035828023901296)
XLA Ops:
  0.0 0.0 copy-start
  0.0 0.9 %copy-done = bf16[2,128,512]{2,1,0:T(8,128)(2,1)S(1)} copy-done((bf16[2,128,512]{2,1,0:T(8,128)(2,1)S(1)}, bf16[2,128,512]{2,1,0:T(8,128)(2,1)}, u32[]{:S(2)}) %copy-start) | copy-done | bytes 262168
  1.0 0.0 copy-start.3
  1.0 0.8 copy-done.3
  1.8 0.0 copy-start.5
  1.8 0.8 copy-done.5
  2.6 0.8 shard_map.46
  3.4 26.5 %all_to_all.20 = bf16[128,4,128]{2,1,0:T(4,128)(2,1)S(1)} all-to-all(bf16[128,4,128]{2,1,0:T(4,128)(2,1)S(1)} %bitcast.19), channel_id=1, replica_groups=mesh['y'=4,'x'=4,'zh'=4,'zl'=2,'c'=2] {'zl','y','x','zh'}, dimensions={0} | all-to-all | bytes 262144 | tf_op jit(solution)/shard_map/all_to_all | solution.py:192
  29.9 0.0 copy-start.1
  29.9 2.2 %collective-permute-start = (bf16[512,128]{1,0:T(8,128)(2,1)S(1)}, bf16[512,128]{1,0:T(8,128)(2,1)S(1)}, u32[]{:S(2)}, u32[]{:S(2)}) collective-permute-start(bf16[512,128]{1,0:T(8,128)(2,1)S(1)} %bitcast.10), channel_id=1, source_target_pairs={{0,1},{1,0},{2,3},{3,2},{4,5},{5,4},{6,7},{7,6},{8,9},{9,8},{10,11... | collective-permute-start | bytes 393224 | tf_op jit(solution)/shard_map/ppermute | solution.py:196
  32.0 1.0 %collective-permute-done.partner = bf16[512,128]{1,0:T(8,128)(2,1)S(1)} collective-permute-done((bf16[512,128]{1,0:T(8,128)(2,1)S(1)}, bf16[512,128]{1,0:T(8,128)(2,1)S(1)}, u32[]{:S(2)}, u32[]{:S(2)}) %collective-permute-start) | collective-permute-done | bytes 131104 | tf_op jit(solution)/shard_map/ppermute | solution.py:196
  33.0 0.7 shard_map.47
  33.7 0.0 copy-start.2
  33.8 0.0 copy-start.4
  33.8 16.1 %all_to_all.21 = bf16[128,2,128]{2,1,0:T(2,128)(2,1)S(1)} all-to-all(bf16[128,2,128]{2,1,0:T(2,128)(2,1)S(1)} %bitcast.15), channel_id=1, replica_groups=mesh['y'=4,'x'=4,'zh'=4,'zl'=2,'c'=2] {'zl','y','x','zh'}, dimensions={0} | all-to-all | bytes 131072 | tf_op jit(solution)/shard_map/all_to_all | solution.py:192
  49.9 0.0 copy-done.1
  49.9 0.0 copy-done.2
  49.9 0.0 copy-done.4
  49.9 1.0 %shard_map.48 = (bf16[512,128]{1,0:T(8,128)(2,1)S(1)}, f32[128,256]{1,0:T(8,128)S(1)}, f32[128,256]{1,0:T(8,128)S(1)}) custom-call(bf16[256,128]{1,0:T(8,128)(2,1)S(1)} %bitcast.17, f32[128,256]{1,0:T(8,128)S(1)} %get-tuple-element.12.state, f32[128,256]{1,0:T(8,128)S(1)} %get-tuple-element.13.gate, bf16[2,128,128]{2,1,0:T(8,128)(2,1)S(1)} %copy-done.2, ...), custom_call_target="tpu_custom_call" | custom-call | tf_op jit(solution)/shard_map/pallas_call | solution.py:181
  50.9 16.2 %all_to_all.22 = bf16[128,4,128]{2,1,0:T(4,128)(2,1)S(1)} all-to-all(bf16[128,4,128]{2,1,0:T(4,128)(2,1)S(1)} %bitcast.18), channel_id=1, replica_groups=mesh['y'=4,'x'=4,'zh'=4,'zl'=2,'c'=2] {'zl','y','x','zh'}, dimensions={0} | all-to-all | bytes 262144 | tf_op jit(solution)/shard_map/all_to_all | solution.py:192
  67.1 3.3 %collective-permute-start.1 = (bf16[512,128]{1,0:T(8,128)(2,1)S(1)}, bf16[512,128]{1,0:T(8,128)(2,1)S(1)}, u32[]{:S(2)}, u32[]{:S(2)}) collective-permute-start(bf16[512,128]{1,0:T(8,128)(2,1)S(1)} %bitcast.12), channel_id=1, source_target_pairs={{0,1},{1,0},{2,3},{3,2},{4,5},{5,4},{6,7},{7,6},{8,9},{9,8},{10,11... | collective-permute-start | bytes 393224 | tf_op jit(solution)/shard_map/ppermute | solution.py:196
  70.4 1.0 %collective-permute-done.1.partner = bf16[512,128]{1,0:T(8,128)(2,1)S(1)} collective-permute-done((bf16[512,128]{1,0:T(8,128)(2,1)S(1)}, bf16[512,128]{1,0:T(8,128)(2,1)S(1)}, u32[]{:S(2)}, u32[]{:S(2)}) %collective-permute-start.1) | collective-permute-done | bytes 131104 | tf_op jit(solution)/shard_map/ppermute | solution.py:196
  71.4 0.8 shard_map.49
  72.2 16.0 %all_to_all.23 = bf16[128,2,128]{2,1,0:T(2,128)(2,1)S(1)} all-to-all(bf16[128,2,128]{2,1,0:T(2,128)(2,1)S(1)} %bitcast.16), channel_id=1, replica_groups=mesh['y'=4,'x'=4,'zh'=4,'zl'=2,'c'=2] {'zl','y','x','zh'}, dimensions={0} | all-to-all | bytes 131072 | tf_op jit(solution)/shard_map/all_to_all | solution.py:192
  88.2 1.2 %shard_map.50 = bf16[256,128]{1,0:T(8,128)(2,1)} custom-call(bf16[256,128]{1,0:T(8,128)(2,1)S(1)} %bitcast.14, f32[128,256]{1,0:T(8,128)S(1)} %get-tuple-element.15.state, f32[128,256]{1,0:T(8,128)S(1)} %get-tuple-element.16.gate, bf16[2,128,128]{2,1,0:T(8,128)(2,1)S(1)} %copy-done.2), custom_call_target="tpu_custom_call" | custom-call | tf_op jit(solution)/shard_map/pallas_call | solution.py:181
Async XLA Ops:
  0.0 0.9 %copy-start = (bf16[2,128,512]{2,1,0:T(8,128)(2,1)S(1)}, bf16[2,128,512]{2,1,0:T(8,128)(2,1)}, u32[]{:S(2)}) copy-start(bf16[2,128,512]{2,1,0:T(8,128)(2,1)} %in_w.3) | copy-start | bytes 786436
  1.0 0.8 copy-start.3
  1.8 0.8 copy-start.5
  29.9 20.0 %copy-start.1 = (bf16[2,128,512]{2,1,0:T(8,128)(2,1)S(1)}, bf16[2,128,512]{2,1,0:T(8,128)(2,1)}, u32[]{:S(2)}) copy-start(bf16[2,128,512]{2,1,0:T(8,128)(2,1)} %in_w.3) | copy-start | bytes 786436
  29.9 3.1 %collective-permute-start = (bf16[512,128]{1,0:T(8,128)(2,1)S(1)}, bf16[512,128]{1,0:T(8,128)(2,1)S(1)}, u32[]{:S(2)}, u32[]{:S(2)}) collective-permute-start(bf16[512,128]{1,0:T(8,128)(2,1)S(1)} %bitcast.10), channel_id=1, source_target_pairs={{0,1},{1,0},{2,3},{3,2},{4,5},{5,4},{6,7},{7,6},{8,9},{9,8},{10,11... | collective-permute-start | bytes 393224 | tf_op jit(solution)/shard_map/ppermute | solution.py:196
  33.7 16.2 %copy-start.2 = (bf16[2,128,128]{2,1,0:T(8,128)(2,1)S(1)}, bf16[2,128,128]{2,1,0:T(8,128)(2,1)}, u32[]{:S(2)}) copy-start(bf16[2,128,128]{2,1,0:T(8,128)(2,1)} %out_w.3) | copy-start | bytes 196612
  33.8 16.2 %copy-start.4 = (bf16[2,128,128]{2,1,0:T(8,128)(2,1)S(1)}, bf16[2,128,128]{2,1,0:T(8,128)(2,1)}, u32[]{:S(2)}) copy-start(bf16[2,128,128]{2,1,0:T(8,128)(2,1)} %gate_w.3) | copy-start | bytes 196612
  67.1 4.3 %collective-permute-start.1 = (bf16[512,128]{1,0:T(8,128)(2,1)S(1)}, bf16[512,128]{1,0:T(8,128)(2,1)S(1)}, u32[]{:S(2)}, u32[]{:S(2)}) collective-permute-start(bf16[512,128]{1,0:T(8,128)(2,1)S(1)} %bitcast.12), channel_id=1, source_target_pairs={{0,1},{1,0},{2,3},{3,2},{4,5},{5,4},{6,7},{7,6},{8,9},{9,8},{10,11... | collective-permute-start | bytes 393224 | tf_op jit(solution)/shard_map/ppermute | solution.py:196

commit v3 on v2

--- a/solution.py
+++ b/solution.py
@@ -10,6 +10,8 @@
 F32 = jnp.float32
 
 CHIPS = ("zl", "y", "x", "zh")
+LAYER = ("y", "x", "zl", "c")
+ALL = ("zh", "zl", "c", "y", "x")
 
 
 def nn(a, b):
@@ -75,15 +77,39 @@
 
 
 def sent_operands(weights, normed):
-    left, right = operands(transposed(weights), normed)
-    parts = [v[:, 128 * r : 128 * r + 128] for v in (left, right) for r in range(2)]
-    return interleaved(parts, 64)
+    weights = transposed(weights)
+    pairs = [operands(weights, normed[128 * r : 128 * r + 128]) for r in range(2)]
+    return interleaved([pair[side] for side in range(2) for pair in pairs], 64)
+
+
+def gated(weights, normed):
+    weights = transposed(weights)
+    return jnp.concatenate(
+        [sigmoid(nn(weights, normed[128 * r : 128 * r + 128])) for r in range(2)], 0
+    )
+
+
+def normalized_halves(values):
+    return jnp.concatenate([normalized(values[0:128]), normalized(values[128:256])], 0)
+
+
+def normalized_mixed(values):
+    def mean(array):
+        total = jnp.sum(array, axis=0)
+        total = total + jnp.roll(total, 4, 0)
+        return (total + jnp.roll(total, 2, 0)) / 128
+
+    tiles = values.reshape(32, 8, 128)
+    shifted = tiles - mean(tiles)
+    scale = lax.rsqrt(mean(shifted * shifted) + EPSILON)
+    return (shifted * scale).reshape(256, 128).astype(BF16)
 
 
 def first_math(own, in_w, gate_w):
-    state = nt(identity(128), own)
-    normed = normalized(state)
-    return sent_operands(in_w, normed), state, sigmoid(nn(transposed(gate_w), normed))
+    eye = identity(128)
+    state = jnp.concatenate([nt(eye, own[0:128]), nt(eye, own[128:256])], 0)
+    normed = normalized_halves(state)
+    return sent_operands(in_w, normed), state, gated(gate_w, normed)
 
 
 def by_core(core, mine, other):
@@ -112,50 +138,75 @@
     return returned(*(nt(jnp.concatenate(v, 1), right) for v in lefts))
 
 
-def residual(gathered, out_w, state, gate):
-    split = nn(picks(256, 256, lambda i: i % 128 * 2 + i // 128), gathered)
-    product = jnp.concatenate([split[0:128], split[128:256]], 1)
-    update = nn(transposed(out_w), normalized(product))
+def residual(product, channel_of, out_w, state, gate):
+    weights = transposed(out_w)
+    row = lax.broadcasted_iota(jnp.int32, (128, 256), 0)
+    col = lax.broadcasted_iota(jnp.int32, (128, 256), 1)
+    spread = []
+    for r in range(2):
+        one_hot = (row == channel_of(col // 2)) & (col % 2 == r)
+        spread.append(moved(weights, one_hot.astype(F32).astype(BF16)))
+    update = nn(jnp.concatenate(spread, 0), normalized_mixed(product))
     return (state + gate * update).astype(BF16)
 
 
 def middle_math(gathered, state, gate, out_w, in_w, gate_w):
-    middle = residual(gathered, out_w, state, gate).astype(F32)
-    normed = normalized(middle)
-    return sent_operands(in_w, normed), middle, sigmoid(nn(transposed(gate_w), normed))
-
-
-def incoming_math(core, received, partner):
-    take_left = picks(128, 256, lambda i: i // 2 * 4 + i % 2)
-    take_right = picks(128, 256, lambda i: i // 2 * 4 + 2 + i % 2)
-    lanes = picks(128, 128, lambda i: i // 64 * 64 + i % 32 * 2 + i % 64 // 32)
-    lefts, rights = {}, []
+    middle = residual(gathered.astype(F32), lambda h: h, out_w, state, gate).astype(F32)
+    normed = normalized_halves(middle)
+    return sent_operands(in_w, normed), middle, gated(gate_w, normed)
+
+
+def incoming_math(received):
+    sides = {}
+    for channel in range(2):
+        for side in range(2):
+            place = 4 * channel + 2 * side
+            take = picks(128, 512, lambda i: i % 32 // 2 * 32 + i // 32 * 8 + place + i % 2)
+            rows = nn(take, received)
+            halves = []
+            for zl in range(2):
+                pair = (rows[64 * zl : 64 * zl + 32], rows[64 * zl + 32 : 64 * zl + 64])
+                halves.append(jnp.concatenate(halves_swapped(*pair), 0))
+            sides[channel, side] = jnp.concatenate(halves, 1).astype(BF16)
+    lefts = []
+    for channel in range(2):
+        row = lax.broadcasted_iota(jnp.int32, (512, 256), 0)
+        col = lax.broadcasted_iota(jnp.int32, (512, 256), 1)
+        source = row % 64 // 4 * 16 + row % 256 // 64 * 4 + row % 2 * 2 + row // 256
+        one_hot = (col == source) & (row // 2 % 2 == channel)
+        lefts.append(nt(one_hot.astype(F32).astype(BF16), sides[channel, 0]).astype(BF16))
+    right = jnp.concatenate([sides[0, 1], sides[1, 1]], 0)
+    total = nn(jnp.concatenate(lefts, 1), right)
+    blocks = []
     for zl in range(2):
-        block = received[256 * zl : 256 * zl + 256]
-        mine = nt(lanes, moved(take_left, block)).astype(BF16)
-        there = moved(take_left, partner[256 * zl : 256 * zl + 256])
-        other = nt(lanes, there).astype(BF16)
-        lefts[zl, 0], lefts[zl, 1] = by_core(core, mine, other)
-        rights.append(nn(take_right, block))
-    right = jnp.concatenate(halves_swapped(*rights), 0).astype(BF16)
-    order = [lefts[zl, c] for zl in range(2) for c in range(2)]
-    totals = []
-    for odd in range(2):
-        rows = [
-            jnp.concatenate([v[32 * odd : 32 * odd + 32], v[64 + 32 * odd : 96 + 32 * odd]], 1)
-            for v in order
-        ]
-        totals.append(nn(jnp.concatenate(rows, 0), right))
-    return returned(*totals)
+        lanes = slice(128 * zl, 128 * zl + 128)
+        blocks.extend(halves_swapped(total[0:256, lanes], total[256:512, lanes]))
+    return jnp.concatenate(
+        [b[64 * zh : 64 * zh + 64] for zh in range(4) for b in blocks], 0
+    ).astype(BF16)
 
 
 def last_math(gathered, state, gate, out_w):
-    refined = residual(gathered, out_w, state, gate)
-    return nt(identity(256), refined).astype(BF16)
-
-
-def first_kernel(own, in_w, gate_w, sent, state, gate):
-    sent[...], state[...], gate[...] = first_math(own[...], in_w[0], gate_w[0])
+    parts = [gathered[256 * zh : 256 * zh + 256].astype(F32) for zh in range(4)]
+    product = parts[0] + parts[1] + parts[2] + parts[3]
+    refined = residual(
+        product, lambda h: h % 32 // 2 * 8 + h // 32 * 2 + h % 2, out_w, state, gate
+    )
+    eye = identity(128)
+    return jnp.concatenate([nt(eye, refined[0:128]), nt(eye, refined[128:256])], 0).astype(BF16)
+
+
+def first_kernel(own_hbm, in_hbm, gate_hbm, sent, state, gate, own, in_w, gate_w, done):
+    copies = [
+        pltpu.make_async_copy(own_hbm, own, done.at[0]),
+        pltpu.make_async_copy(in_hbm.at[0], in_w, done.at[1]),
+        pltpu.make_async_copy(gate_hbm.at[0], gate_w, done.at[2]),
+    ]
+    for copy in copies:
+        copy.start()
+    for copy in copies:
+        copy.wait()
+    sent[...], state[...], gate[...] = first_math(own[...], in_w[...], gate_w[...])
 
 
 def outgoing_kernel(received, partner, sent):
@@ -168,28 +219,29 @@
     )
 
 
-def incoming_kernel(received, partner, sent):
-    sent[...] = incoming_math(lax.axis_index("c"), received[...], partner[...])
+def incoming_kernel(received, sent):
+    sent[...] = incoming_math(received[...])
 
 
 def last_kernel(gathered, state, gate, out_w, refined):
     refined[...] = last_math(gathered[...], state[...], gate[...], out_w[1])
 
 
-def call(kernel, outs, *arrays):
+def call(kernel, outs, *arrays, space=pltpu.VMEM, scratch=()):
     vmem = pl.BlockSpec(memory_space=pltpu.VMEM)
     return pl.pallas_call(
         kernel,
         out_shape=tuple(jax.ShapeDtypeStruct(shape, dtype) for shape, dtype in outs),
-        in_specs=[vmem] * len(arrays),
+        in_specs=[pl.BlockSpec(memory_space=space)] * len(arrays),
         out_specs=tuple(vmem for _ in outs),
+        scratch_shapes=scratch,
         compiler_params=pltpu.CompilerParams(vmem_limit_bytes=16 << 20),
     )(*arrays)
 
 
-def exchanged(rows):
-    blocks = rows.reshape(128, -1, 128)
-    return lax.all_to_all(blocks, CHIPS, 0, 0, tiled=True).reshape(rows.shape)
+def exchanged(rows, axes):
+    blocks = rows.reshape(lax.axis_size(axes), -1, 128)
+    return lax.all_to_all(blocks, axes, 0, 0, tiled=True).reshape(rows.shape)
 
 
 def from_partner(value):
@@ -198,20 +250,28 @@
 
 def per_device(pair_rep, in_weights, gate_weights, out_weights):
     own = pair_rep.reshape(256, 128)
-    operands_out, results_out = ((512, 128), BF16), ((256, 128), BF16)
-    kept = ((128, 256), F32)
+    kept = ((256, 128), F32)
+    sources = [
+        pltpu.with_memory_space_constraint(v, pltpu.HBM) for v in (own, in_weights, gate_weights)
+    ]
     sent, state, gate = call(
-        first_kernel, [operands_out, kept, kept], own, in_weights, gate_weights
-    )
-    received = exchanged(sent)
-    (sent,) = call(outgoing_kernel, [results_out], received, from_partner(received))
+        first_kernel, [((512, 128), BF16), kept, kept], *sources,
+        space=pltpu.HBM,
+        scratch=[
+            pltpu.VMEM((256, 128), BF16), pltpu.VMEM((128, 512), BF16),
+            pltpu.VMEM((128, 128), BF16), pltpu.SemaphoreType.DMA((3,)),
+        ],
+    )
+    received = exchanged(sent, CHIPS)
+    (sent,) = call(outgoing_kernel, [((256, 128), BF16)], received, from_partner(received))
     sent, state, gate = call(
-        middle_kernel, [operands_out, kept, kept],
-        exchanged(sent), state, gate, out_weights, in_weights, gate_weights,
-    )
-    received = exchanged(sent)
-    (sent,) = call(incoming_kernel, [results_out], received, from_partner(received))
-    (refined,) = call(last_kernel, [results_out], exchanged(sent), state, gate, out_weights)
+        middle_kernel, [((512, 128), BF16), kept, kept],
+        exchanged(sent, CHIPS), state, gate, out_weights, in_weights, gate_weights,
+    )
+    (sent,) = call(incoming_kernel, [((1024, 128), BF16)], exchanged(sent, LAYER))
+    (refined,) = call(
+        last_kernel, [((256, 128), BF16)], exchanged(sent, ALL), state, gate, out_weights
+    )
     return refined.reshape(pair_rep.shape)
 
 

time: 89.7 us -> 87.6 us (0.977)
  blocking collectives: 74.8 us -> 78.4 us
  starting transfers between devices: 5.42 us -> 2.15 us
  local copies, waits for them, and re-layouts: 2.64 us -> 0.02 us
  Pallas kernels: 4.48 us -> 5.73 us
  waiting for transfers between devices: 1.97 us -> 0.99 us
    all_to_all x4, blocking collectives: 74.8 us -> 78.4 us  [exchanged(): return lax.all_to_all(blocks, axes, 0, 0, tiled=True).reshape(rows.shape)]
    ppermute x2 -> x1, starting transfers between devices: 5.42 us -> 2.15 us  [from_partner(): return lax.ppermute(value, 'c', [(0, 1), (1, 0)])]
    unnamed x12 -> x6, local copies, waits for them, and re-layouts: 2.64 us -> 0.02 us
    pallas_call x5, Pallas kernels: 4.48 us -> 5.73 us  [call(): pl.pallas_call(kernel, out_shape=tuple((jax.ShapeDtypeStruct(shape, dtype...]
    ppermute x2 -> x1, waiting for transfers between devices: 1.97 us -> 0.99 us  [from_partner(): return lax.ppermute(value, 'c', [(0, 1), (1, 0)])]
  transfers between devices with their start and end apart: 2 -> 1, of which waited for: 2 -> 1; matrix products, arithmetic and copies ran while one was open for 0% -> 0% of each run, Pallas kernels for 0% -> 0%
where the time goes in v3:
time: 87.6 us; the launch traced here: 87.4 us
  blocking collectives  78.4 us (89%)
  Pallas kernels  5.73 us (7%)
  starting transfers between devices  2.15 us (2%)
  waiting for transfers between devices  0.99 us (1%)
    all_to_all x4, blocking collectives, exchanged(): return lax.all_to_all(blocks, axes, 0, 0, tiled=True).reshape(rows.shape)  78.4 us
    pallas_call x5, Pallas kernels, call(): pl.pallas_call(kernel, out_shape=tuple((jax.ShapeDtypeStruct(shape, dtype...  5.73 us
    ppermute x1, starting transfers between devices, from_partner(): return lax.ppermute(value, 'c', [(0, 1), (1, 0)])  2.15 us
  transfers between devices with their start and end apart: 1, of which 1 were waited for; matrix products, arithmetic and copies ran while one was open for 0% of the time, Pallas kernels for 0%

profile of v3, /device:TPU:1, one launch (start us, length us, event | category | flops | bytes accessed | tf_op | source)
XLA Modules:
  0.0 87.4 jit_solution(2814326461948185074)
XLA Ops:
  0.0 1.8 %shard_map.46 = (bf16[512,128]{1,0:T(8,128)(2,1)S(1)}, f32[256,128]{1,0:T(8,128)S(1)}, f32[256,128]{1,0:T(8,128)S(1)}) custom-call(bf16[256,128]{1,0:T(8,128)(2,1)} %bitcast.19, bf16[2,128,512]{2,1,0:T(8,128)(2,1)} %in_w.1, bf16[2,128,128]{2,1,0:T(8,128)(2,1)} %gate_w.1), custom_call_target="tpu_custom_call" | custom-call | tf_op jit(solution)/shard_map/pallas_call | solution.py:232
  1.8 26.5 %all_to_all.20 = bf16[128,4,128]{2,1,0:T(4,128)(2,1)S(1)} all-to-all(bf16[128,4,128]{2,1,0:T(4,128)(2,1)S(1)} %bitcast.18), channel_id=1, replica_groups=mesh['y'=4,'x'=4,'zh'=4,'zl'=2,'c'=2] {'zl','y','x','zh'}, dimensions={0} | all-to-all | bytes 262144 | tf_op jit(solution)/shard_map/all_to_all | solution.py:244
  28.3 0.0 copy-start
  28.3 2.2 %collective-permute-start = (bf16[512,128]{1,0:T(8,128)(2,1)S(1)}, bf16[512,128]{1,0:T(8,128)(2,1)S(1)}, u32[]{:S(2)}, u32[]{:S(2)}) collective-permute-start(bf16[512,128]{1,0:T(8,128)(2,1)S(1)} %bitcast.13), channel_id=1, source_target_pairs={{0,1},{1,0},{2,3},{3,2},{4,5},{5,4},{6,7},{7,6},{8,9},{9,8},{10,11... | collective-permute-start | bytes 393224 | tf_op jit(solution)/shard_map/ppermute | solution.py:248
  30.4 1.0 %collective-permute-done.partner = bf16[512,128]{1,0:T(8,128)(2,1)S(1)} collective-permute-done((bf16[512,128]{1,0:T(8,128)(2,1)S(1)}, bf16[512,128]{1,0:T(8,128)(2,1)S(1)}, u32[]{:S(2)}, u32[]{:S(2)}) %collective-permute-start) | collective-permute-done | bytes 131104 | tf_op jit(solution)/shard_map/ppermute | solution.py:248
  31.4 0.7 shard_map.47
  32.1 0.0 copy-start.1
  32.2 0.0 copy-start.2
  32.2 16.1 %all_to_all.21 = bf16[128,2,128]{2,1,0:T(2,128)(2,1)S(1)} all-to-all(bf16[128,2,128]{2,1,0:T(2,128)(2,1)S(1)} %bitcast.15), channel_id=1, replica_groups=mesh['y'=4,'x'=4,'zh'=4,'zl'=2,'c'=2] {'zl','y','x','zh'}, dimensions={0} | all-to-all | bytes 131072 | tf_op jit(solution)/shard_map/all_to_all | solution.py:244
  48.3 0.0 copy-done
  48.3 0.0 copy-done.1
  48.3 0.0 copy-done.2
  48.3 1.1 %shard_map.48 = (bf16[512,128]{1,0:T(8,128)(2,1)S(1)}, f32[256,128]{1,0:T(8,128)S(1)}, f32[256,128]{1,0:T(8,128)S(1)}) custom-call(bf16[256,128]{1,0:T(8,128)(2,1)S(1)} %bitcast.16, f32[256,128]{1,0:T(8,128)S(1)} %get-tuple-element.12.state, f32[256,128]{1,0:T(8,128)S(1)} %get-tuple-element.13.gate, bf16[2,128,128]{2,1,0:T(8,128)(2,1)S(1)} %copy-done.1, ...), custom_call_target="tpu_custom_call" | custom-call | tf_op jit(solution)/shard_map/pallas_call | solution.py:232
  49.4 14.7 %all_to_all.22 = bf16[64,8,128]{2,1,0:T(8,128)(2,1)S(1)} all-to-all(bf16[64,8,128]{2,1,0:T(8,128)(2,1)S(1)} %bitcast.17), channel_id=1, replica_groups=mesh['y'=4,'x'=4,'zh'=4,'zl'=2,'c'=2] {'y','x','zl','c'}, dimensions={0} | all-to-all | bytes 262144 | tf_op jit(solution)/shard_map/all_to_all | solution.py:244
  64.1 0.9 %shard_map.49 = bf16[1024,128]{1,0:T(8,128)(2,1)S(1)} custom-call(bf16[512,128]{1,0:T(8,128)(2,1)S(1)} %bitcast.12), custom_call_target="tpu_custom_call" | custom-call | tf_op jit(solution)/shard_map/pallas_call | solution.py:232
  65.1 21.1 %all_to_all.23 = bf16[256,4,128]{2,1,0:T(4,128)(2,1)S(1)} all-to-all(bf16[256,4,128]{2,1,0:T(4,128)(2,1)S(1)} %bitcast.11), channel_id=1, replica_groups=mesh['y'=4,'x'=4,'zh'=4,'zl'=2,'c'=2] {'zh','zl','c','y','x'}, dimensions={0} | all-to-all | bytes 524288 | tf_op jit(solution)/shard_map/all_to_all | solution.py:244
  86.1 1.2 %shard_map.50 = bf16[256,128]{1,0:T(8,128)(2,1)} custom-call(bf16[1024,128]{1,0:T(8,128)(2,1)S(1)} %bitcast.10, f32[256,128]{1,0:T(8,128)S(1)} %get-tuple-element.15.state, f32[256,128]{1,0:T(8,128)S(1)} %get-tuple-element.16.gate, bf16[2,128,128]{2,1,0:T(8,128)(2,1)S(1)} %copy-done.1), custom_call_target="tpu_custom_call" | custom-call | tf_op jit(solution)/shard_map/pallas_call | solution.py:232
Async XLA Ops:
  28.3 20.0 %copy-start = (bf16[2,128,512]{2,1,0:T(8,128)(2,1)S(1)}, bf16[2,128,512]{2,1,0:T(8,128)(2,1)}, u32[]{:S(2)}) copy-start(bf16[2,128,512]{2,1,0:T(8,128)(2,1)} %in_w.1) | copy-start | bytes 786436
  28.3 3.1 %collective-permute-start = (bf16[512,128]{1,0:T(8,128)(2,1)S(1)}, bf16[512,128]{1,0:T(8,128)(2,1)S(1)}, u32[]{:S(2)}, u32[]{:S(2)}) collective-permute-start(bf16[512,128]{1,0:T(8,128)(2,1)S(1)} %bitcast.13), channel_id=1, source_target_pairs={{0,1},{1,0},{2,3},{3,2},{4,5},{5,4},{6,7},{7,6},{8,9},{9,8},{10,11... | collective-permute-start | bytes 393224 | tf_op jit(solution)/shard_map/ppermute | solution.py:248
  32.1 16.2 %copy-start.1 = (bf16[2,128,128]{2,1,0:T(8,128)(2,1)S(1)}, bf16[2,128,128]{2,1,0:T(8,128)(2,1)}, u32[]{:S(2)}) copy-start(bf16[2,128,128]{2,1,0:T(8,128)(2,1)} %out_w.3) | copy-start | bytes 196612
  32.2 16.2 %copy-start.2 = (bf16[2,128,128]{2,1,0:T(8,128)(2,1)S(1)}, bf16[2,128,128]{2,1,0:T(8,128)(2,1)}, u32[]{:S(2)}) copy-start(bf16[2,128,128]{2,1,0:T(8,128)(2,1)} %gate_w.1) | copy-start | bytes 196612

commit v4 on v3

v4 whole, which is shorter than its diff:
```python
import jax
import jax.numpy as jnp
import numpy as np
from jax import lax
from jax.experimental import pallas as pl
from jax.experimental.pallas import tpu as pltpu
from jax.sharding import Mesh, PartitionSpec as P

EPSILON = 1e-05
BF16 = jnp.bfloat16
F32 = jnp.float32

CHIPS = ("zl", "y", "x", "zh")
TO_OWNERS = ("zl", "c", "y", "x", "zh")
LAYER = ("zl", "c", "y", "x")
FROM_LAYER = ("zh", "zl", "c", "y", "x")


def nn(a, b):
    return lax.dot_general(a, b, (((1,), (0,)), ((), ())), preferred_element_type=F32)


def nt(a, b):
    return lax.dot_general(a, b, (((1,), (1,)), ((), ())), preferred_element_type=F32)


def moved(one_hot, values):
    return nn(one_hot, values).astype(BF16)


def one_hot(rows, cols, source, valid=lambda i: i >= 0):
    index = np.arange(rows)
    hits = np.arange(cols)[None, :] == np.where(valid(index), source(index), -1)[:, None]
    return hits.astype(jnp.bfloat16)


DEAL = one_hot(256, 256, lambda i: i % 4 * 64 + i // 4)
SIDES = one_hot(256, 256, lambda i: i % 128 // 2 * 4 + i // 128 * 2 + i % 2)
ROWS = one_hot(256, 256, lambda i: i % 2 * 128 + i // 2)
TAKE = one_hot(128, 128, lambda i: i % 16 * 8 + i // 16)
TARGETS = np.stack(
    [
        one_hot(
            512, 256,
            lambda i: i % 64 // 4 * 16 + i % 256 // 64 * 4 + i % 2 * 2 + i // 256,
            lambda i: i // 2 % 2 == channel,
        )
        for channel in range(2)
    ]
)
SPREAD = np.stack(
    [one_hot(256, 128, lambda i: i // 2, lambda i: i % 2 == r).T for r in range(2)]
)
EYE = one_hot(128, 128, lambda i: i)


def normalized(values):
    tiles = values.reshape(-1, 128, 128)
    shifted = tiles - jnp.mean(tiles, axis=1, keepdims=True)
    spread = jnp.mean(shifted * shifted, axis=1, keepdims=True)
    return (shifted * lax.rsqrt(spread + EPSILON)).reshape(values.shape).astype(BF16)


def normalized_mixed(values):
    def mean(array):
        total = jnp.sum(array, axis=0)
        total = total + jnp.roll(total, 4, 0)
        return (total + jnp.roll(total, 2, 0)) / 128

    tiles = values.reshape(32, 8, 128)
    shifted = tiles - mean(tiles)
    scale = lax.rsqrt(mean(shifted * shifted) + EPSILON)
    return (shifted * scale).reshape(256, 128).astype(BF16)


def sigmoid(x):
    return 1.0 / (1.0 + jnp.exp(-x))


def halves_swapped(a, b):
    low = lax.broadcasted_iota(jnp.int32, a.shape, 1) < 64
    return jnp.where(low, a, jnp.roll(b, 64, 1)), jnp.where(low, jnp.roll(a, 64, 1), b)


def transposed(weights, eye):
    blocks = [nt(eye, weights[:, k : k + 128]) for k in range(0, weights.shape[1], 128)]
    return jnp.concatenate(blocks, 0).astype(BF16)


def sent_operands(weights, normed, deal):
    parts = []
    for r in range(2):
        projected = nn(weights, normed[128 * r : 128 * r + 128])
        for side in range(2):
            gate, value = (projected[k : k + 128] for k in (256 * side, 256 * side + 128))
            parts.append((sigmoid(gate) * value).astype(BF16))
    parts = [parts[k] for k in (0, 2, 1, 3)]
    return jnp.concatenate(
        [moved(deal, jnp.concatenate([p[k : k + 64] for p in parts], 0)) for k in (0, 64)], 0
    )


def gates(weights, state):
    normed = normalized(state)
    return jnp.concatenate([sigmoid(nn(weights, normed[k : k + 128])) for k in (0, 128)], 0)


def residual(product, spread_w, state, gate):
    update = nn(spread_w, normalized_mixed(product))
    return (state + gate * update).astype(BF16)


def first_math(own, in_w, eye, deal):
    state = jnp.concatenate([nt(eye, own[0:128]), nt(eye, own[128:256])], 0)
    return sent_operands(transposed(in_w, eye), normalized(state), deal), state


def side_math(state, in_w, gate_w, out_w, eye, spread):
    gate_t = [transposed(gate_w[u], eye) for u in range(2)]
    out_t = [transposed(out_w[u], eye) for u in range(2)]
    spread_w = [jnp.concatenate([moved(t, spread[r]) for r in range(2)], 0) for t in out_t]
    return gates(gate_t[0], state), transposed(in_w[1], eye), gate_t[1], *spread_w


def outgoing_math(received, sides, rows):
    split = [nn(sides, received[256 * zl : 256 * zl + 256]) for zl in range(2)]
    left = [v.astype(BF16) for v in halves_swapped(split[0][0:128], split[1][0:128])]
    right = jnp.concatenate(halves_swapped(split[0][128:256], split[1][128:256]), 0)
    right = moved(rows, right.astype(BF16))
    even, odd = (nt(v, right) for v in left)
    blocks = []
    for k in (0, 128):
        blocks.extend(halves_swapped(even[:, k : k + 128], odd[:, k : k + 128]))
    return jnp.concatenate(blocks, 0).astype(BF16)


def middle_math(gathered, state, gate, spread_w, in_t, deal):
    parts = gathered.astype(F32).reshape(2, 2, 128, 128)
    product = (parts[:, 0] + parts[:, 1]).reshape(256, 128)
    middle = residual(product, spread_w, state, gate).astype(F32)
    return sent_operands(in_t, normalized(middle), deal), middle


def incoming_math(received, take, targets):
    blocks = [nn(take, received[128 * ka : 128 * ka + 128]) for ka in range(4)]
    swapped = [halves_swapped(blocks[0], blocks[1]), halves_swapped(blocks[2], blocks[3])]

    def side_of(place):
        rows = slice(32 * place, 32 * place + 32)
        return jnp.concatenate(
            [jnp.concatenate([half[rows] for half in pair], 0) for pair in swapped], 1
        ).astype(BF16)

    lefts = [nt(targets[channel], side_of(2 * channel)).astype(BF16) for channel in range(2)]
    right = jnp.concatenate([side_of(1), side_of(3)], 0)
    total = nn(jnp.concatenate(lefts, 1), right)
    blocks = []
    for k in (0, 128):
        blocks.extend(halves_swapped(total[0:256, k : k + 128], total[256:512, k : k + 128]))
    return jnp.concatenate(
        [b[64 * zh : 64 * zh + 64] for zh in range(4) for b in blocks], 0
    ).astype(BF16)


def last_math(gathered, state, gate, spread_w, eye):
    product = jnp.sum(gathered.astype(F32).reshape(4, 256, 128), axis=0)
    refined = residual(product, spread_w, state, gate)
    return jnp.concatenate([nt(eye, refined[0:128]), nt(eye, refined[128:256])], 0).astype(BF16)


def first_kernel(own_hbm, in_hbm, eye_hbm, deal_hbm, sent, state, own, in_w, eye, deal, done):
    copies = [
        pltpu.make_async_copy(source, target, done.at[k])
        for k, (source, target) in enumerate(
            ((own_hbm, own), (in_hbm.at[0], in_w), (eye_hbm, eye), (deal_hbm, deal))
        )
    ]
    for copy in copies:
        copy.start()
    for copy in copies:
        copy.wait()
    sent[...], state[...] = first_math(own[...], in_w[...], eye[...], deal[...])


def side_kernel(state, in_w, gate_w, out_w, eye, spread, gate, in_t, gate_t, spread_0, spread_1):
    gate[...], in_t[...], gate_t[...], spread_0[...], spread_1[...] = side_math(
        state[...], in_w[...], gate_w[...], out_w[...], eye[...], spread[...]
    )


def outgoing_kernel(received, sides, rows, sent):
    sent[...] = outgoing_math(received[...], sides[...], rows[...])


def middle_kernel(gathered, state, gate, spread_w, in_t, deal, sent, middle):
    sent[...], middle[...] = middle_math(
        gathered[...], state[...], gate[...], spread_w[...], in_t[...], deal[...]
    )


def gate_kernel(gate_t, state, gate):
    gate[...] = gates(gate_t[...], state[...])


def incoming_kernel(received, take, targets, sent):
    sent[...] = incoming_math(received[...], take[...], targets[...])


def last_kernel(gathered, state, gate, spread_w, eye, refined):
    refined[...] = last_math(gathered[...], state[...], gate[...], spread_w[...], eye[...])


def call(kernel, outs, *arrays, space=pltpu.VMEM, scratch=()):
    vmem = pl.BlockSpec(memory_space=pltpu.VMEM)
    results = pl.pallas_call(
        kernel,
        out_shape=tuple(jax.ShapeDtypeStruct(shape, dtype) for shape, dtype in outs),
        in_specs=[pl.BlockSpec(memory_space=space)] * len(arrays),
        out_specs=tuple(vmem for _ in outs),
        scratch_shapes=scratch,
        compiler_params=pltpu.CompilerParams(vmem_limit_bytes=16 << 20),
        cost_estimate=pl.CostEstimate(flops=400_000_000, bytes_accessed=1 << 20, transcendentals=0),
    )(*arrays)
    return results if len(results) > 1 else results[0]


def exchanged(rows, axes):
    blocks = rows.reshape(lax.axis_size(axes), -1, 128)
    return lax.all_to_all(blocks, axes, 0, 0, tiled=True).reshape(rows.shape)


def per_device(pair_rep, in_weights, gate_weights, out_weights):
    eye, deal = jnp.asarray(EYE), jnp.asarray(DEAL)
    kept = ((256, 128), F32)
    wide = ((256, 256), BF16)
    inputs = [pair_rep.reshape(256, 128), in_weights, eye, deal]
    sent, state = call(
        first_kernel, [((512, 128), BF16), kept],
        *(pltpu.with_memory_space_constraint(v, pltpu.HBM) for v in inputs),
        space=pltpu.HBM,
        scratch=[
            pltpu.VMEM((256, 128), BF16), pltpu.VMEM((128, 512), BF16),
            pltpu.VMEM((128, 128), BF16), pltpu.VMEM((256, 256), BF16),
            pltpu.SemaphoreType.DMA((4,)),
        ],
    )
    gate, in_t, gate_t, spread_0, spread_1 = call(
        side_kernel, [kept, ((512, 128), BF16), ((128, 128), BF16), wide, wide],
        state, in_weights, gate_weights, out_weights, eye, jnp.asarray(SPREAD),
    )
    sent = call(
        outgoing_kernel, [((512, 128), BF16)],
        exchanged(sent, CHIPS), jnp.asarray(SIDES), jnp.asarray(ROWS),
    )
    sent, state = call(
        middle_kernel, [((512, 128), BF16), kept],
        exchanged(sent, TO_OWNERS), state, gate, spread_0, in_t, deal,
    )
    gate = call(gate_kernel, [kept], gate_t, state)
    sent = call(
        incoming_kernel, [((1024, 128), BF16)],
        exchanged(sent, LAYER), jnp.asarray(TAKE), jnp.asarray(TARGETS),
    )
    refined = call(
        last_kernel, [((256, 128), BF16)],
        exchanged(sent, FROM_LAYER), state, gate, spread_1, eye,
    )
    return refined.reshape(pair_rep.shape)


def solution(mesh):
    fine = Mesh(mesh.devices.reshape(4, 4, 4, 2, 2), ("y", "x", "zh", "zl", "c"))
    placed = P(("y", "x", "zh"), ("zl", "c"), None)
    return jax.shard_map(
        per_device, mesh=fine, in_specs=(placed, P(), P(), P()), out_specs=placed, check_vma=False
    )
```

time: 87.6 us -> 88.1 us (level)
  blocking collectives: 78.4 us -> 39.6 us
  waiting for transfers between devices: 0.99 us -> 27.9 us
  starting transfers between devices: 2.15 us -> 12.9 us
  Pallas kernels: 5.73 us -> 7.17 us
    all_to_all x4 -> x2, blocking collectives: 78.4 us -> 39.6 us  [exchanged(): return lax.all_to_all(blocks, axes, 0, 0, tiled=True).reshape(rows.shape)]
    all_to_all x0 -> x2, waiting for transfers between devices: none -> 27.9 us  [exchanged(): return lax.all_to_all(blocks, axes, 0, 0, tiled=True).reshape(rows.shape)]
    all_to_all x0 -> x2, starting transfers between devices: none -> 12.9 us  [exchanged(): return lax.all_to_all(blocks, axes, 0, 0, tiled=True).reshape(rows.shape)]
    ppermute x1 -> x0, starting transfers between devices: 2.15 us -> none  [from_partner(): return lax.ppermute(value, 'c', [(0, 1), (1, 0)])]
    pallas_call x5 -> x7, Pallas kernels: 5.73 us -> 7.17 us  [call(): pl.pallas_call(kernel, out_shape=tuple((jax.ShapeDtypeStruct(shape, dtype...]
    ppermute x1 -> x0, waiting for transfers between devices: 0.99 us -> none  [from_partner(): return lax.ppermute(value, 'c', [(0, 1), (1, 0)])]
  transfers between devices with their start and end apart: 1 -> 2, of which waited for: 1 -> 2; matrix products, arithmetic and copies ran while one was open for 0% -> 0% of each run, Pallas kernels for 0% -> 1%
where the time goes in v4:
time: 88.1 us; the launch traced here: 87.8 us
  blocking collectives  39.6 us (45%)
  waiting for transfers between devices  27.9 us (32%)
  starting transfers between devices  12.9 us (15%)
  Pallas kernels  7.17 us (8%)
    all_to_all x2, blocking collectives, exchanged(): return lax.all_to_all(blocks, axes, 0, 0, tiled=True).reshape(rows.shape)  39.6 us
    all_to_all x2, waiting for transfers between devices, exchanged(): return lax.all_to_all(blocks, axes, 0, 0, tiled=True).reshape(rows.shape)  27.9 us
    all_to_all x2, starting transfers between devices, exchanged(): return lax.all_to_all(blocks, axes, 0, 0, tiled=True).reshape(rows.shape)  12.9 us
    pallas_call x7, Pallas kernels, call(): pl.pallas_call(kernel, out_shape=tuple((jax.ShapeDtypeStruct(shape, dtype...  7.17 us
  transfers between devices with their start and end apart: 2, of which 2 were waited for; matrix products, arithmetic and copies ran while one was open for 0% of the time, Pallas kernels for 1%

profile of v4, /device:TPU:1, one launch (start us, length us, event | category | flops | bytes accessed | tf_op | source)
XLA Modules:
  0.0 87.8 jit_solution(11740519108911777763)
XLA Ops:
  0.0 1.7 %shard_map.109 = (bf16[512,128]{1,0:T(8,128)(2,1)S(1)}, f32[256,128]{1,0:T(8,128)S(1)}) custom-call(bf16[256,128]{1,0:T(8,128)(2,1)} %bitcast.16, bf16[2,128,512]{2,1,0:T(8,128)(2,1)} %in_w.1, bf16[128,128]{1,0:T(8,128)(2,1)} %constant.14.clone.eye_hbm.eye, bf16[256,256]{1,0:T(8,128)(2,1)} %constant.15.clone.deal_hbm.deal), custom_call_target="tpu_custom_call" | custom-call | flops 400000000 | bytes 1048576 | tf_op jit(solution)/shard_map/pallas_call | solution.py:215
  1.7 0.0 copy-start.6
  1.7 0.0 copy-start.7
  1.7 26.6 %all_to_all.20 = bf16[128,4,128]{2,1,0:T(4,128)(2,1)S(1)} all-to-all(bf16[128,4,128]{2,1,0:T(4,128)(2,1)S(1)} %bitcast.15), channel_id=1, replica_groups=mesh['y'=4,'x'=4,'zh'=4,'zl'=2,'c'=2] {'zl','y','x','zh'}, dimensions={0} | all-to-all | bytes 262144 | tf_op jit(solution)/shard_map/all_to_all | solution.py:229
  28.4 0.0 copy-done.6
  28.4 0.0 copy-done.7
  28.4 0.0 copy-start.1
  28.4 0.0 copy-start.2
  28.4 0.0 copy-start.5
  28.4 0.0 copy-start.8
  28.4 1.4 %shard_map.110 = bf16[512,128]{1,0:T(8,128)(2,1)} custom-call(bf16[512,128]{1,0:T(8,128)(2,1)S(1)} %bitcast.13, bf16[256,256]{1,0:T(8,128)(2,1)S(1)} %copy-done.7, bf16[256,256]{1,0:T(8,128)(2,1)S(1)} %copy-done.6), custom_call_target="tpu_custom_call" | custom-call | flops 400000000 | bytes 1048576 | tf_op jit(solution)/shard_map/pallas_call | solution.py:215
  29.8 0.0 copy-start
  29.8 7.3 %all-to-all-start.1 = ((bf16[256,2,128]{2,1,0:T(2,128)(2,1)}), bf16[256,2,128]{2,1,0:T(2,128)(2,1)S(1)}, u32[]{:S(2)}, u32[]{:S(2)}) async-start(bf16[256,2,128]{2,1,0:T(2,128)(2,1)} %bitcast.3), calls=%async_computation.1 | async-start | bytes 262144 | tf_op jit(solution)/shard_map/all_to_all | solution.py:229
  37.0 0.0 copy-done.1
  37.1 0.0 copy-done.2
  37.1 0.0 copy-done.5
  37.1 0.0 copy-done.8
  37.1 0.0 copy-done
  37.1 0.0 copy-start.4
  37.1 0.5 shard_map.111
  37.6 12.4 %all-to-all-done.1 = bf16[256,2,128]{2,1,0:T(2,128)(2,1)S(1)} async-done(((bf16[256,2,128]{2,1,0:T(2,128)(2,1)}), bf16[256,2,128]{2,1,0:T(2,128)(2,1)S(1)}, u32[]{:S(2)}, u32[]{:S(2)}) %all-to-all-start.1) | async-done | bytes 131104 | tf_op jit(solution)/shard_map/all_to_all | solution.py:229
  50.0 0.0 copy-done.4
  50.0 0.0 copy-start.3
  50.0 0.7 shard_map.112
  50.7 0.0 copy-start.9
  50.7 13.0 %all_to_all.21 = bf16[64,8,128]{2,1,0:T(8,128)(2,1)S(1)} all-to-all(bf16[64,8,128]{2,1,0:T(8,128)(2,1)S(1)} %bitcast.12), channel_id=1, replica_groups=mesh['y'=4,'x'=4,'zh'=4,'zl'=2,'c'=2] {'zl','c','y','x'}, dimensions={0} | all-to-all | bytes 262144 | tf_op jit(solution)/shard_map/all_to_all | solution.py:229
  63.8 0.0 copy-done.3
  63.8 0.0 copy-done.9
  63.8 1.5 %shard_map.113 = bf16[1024,128]{1,0:T(8,128)(2,1)} custom-call(bf16[512,128]{1,0:T(8,128)(2,1)S(1)} %bitcast.14, bf16[128,128]{1,0:T(8,128)(2,1)S(1)} %copy-done.9, bf16[2,512,256]{2,1,0:T(8,128)(2,1)S(1)} %copy-done.3), custom_call_target="tpu_custom_call" | custom-call | flops 400000000 | bytes 1048576 | tf_op jit(solution)/shard_map/pallas_call | solution.py:215
  65.3 5.6 %all-to-all-start.3 = ((bf16[256,4,128]{2,1,0:T(4,128)(2,1)}), bf16[256,4,128]{2,1,0:T(4,128)(2,1)S(1)}, u32[]{:S(2)}, u32[]{:S(2)}) async-start(bf16[256,4,128]{2,1,0:T(4,128)(2,1)} %bitcast.7), calls=%async_computation.3 | async-start | bytes 524288 | tf_op jit(solution)/shard_map/all_to_all | solution.py:229
  70.9 0.2 shard_map.114.gate
  71.2 15.6 %all-to-all-done.3 = bf16[256,4,128]{2,1,0:T(4,128)(2,1)S(1)} async-done(((bf16[256,4,128]{2,1,0:T(4,128)(2,1)}), bf16[256,4,128]{2,1,0:T(4,128)(2,1)S(1)}, u32[]{:S(2)}, u32[]{:S(2)}) %all-to-all-start.3) | async-done | bytes 262176 | tf_op jit(solution)/shard_map/all_to_all | solution.py:229
  86.8 1.1 %shard_map.115 = bf16[256,128]{1,0:T(8,128)(2,1)} custom-call(bf16[1024,128]{1,0:T(8,128)(2,1)S(1)} %bitcast.10, f32[256,128]{1,0:T(8,128)S(1)} %get-tuple-element.20.state, f32[256,128]{1,0:T(8,128)S(1)} %shard_map.114.gate, bf16[256,256]{1,0:T(8,128)(2,1)S(1)} %get-tuple-element.22.spread_w, bf16[128,128]{1,0:T(8,128)(2,1)S(1)} %copy-done.8), custom_call_target="tpu_custom_call" | custom-call | flops 400000000 | bytes 1048576 | tf_op jit(solution)/shard_map/pallas_call | solution.py:215
Async XLA Ops:
  1.7 26.6 %copy-start.6 = (bf16[256,256]{1,0:T(8,128)(2,1)S(1)}, bf16[256,256]{1,0:T(8,128)(2,1)}, u32[]{:S(2)}) copy-start(bf16[256,256]{1,0:T(8,128)(2,1)} %constant.18.clone.rows) | copy-start | bytes 393220
  1.7 26.6 %copy-start.7 = (bf16[256,256]{1,0:T(8,128)(2,1)S(1)}, bf16[256,256]{1,0:T(8,128)(2,1)}, u32[]{:S(2)}) copy-start(bf16[256,256]{1,0:T(8,128)(2,1)} %constant.17.clone.sides) | copy-start | bytes 393220
  28.4 8.7 %copy-start.1 = (bf16[2,128,128]{2,1,0:T(8,128)(2,1)S(1)}, bf16[2,128,128]{2,1,0:T(8,128)(2,1)}, u32[]{:S(2)}) copy-start(bf16[2,128,128]{2,1,0:T(8,128)(2,1)} %gate_w.1) | copy-start | bytes 196612
  28.4 8.7 %copy-start.2 = (bf16[2,128,128]{2,1,0:T(8,128)(2,1)S(1)}, bf16[2,128,128]{2,1,0:T(8,128)(2,1)}, u32[]{:S(2)}) copy-start(bf16[2,128,128]{2,1,0:T(8,128)(2,1)} %out_w.1) | copy-start | bytes 196612
  28.4 8.7 %copy-start.5 = (bf16[2,128,256]{2,1,0:T(8,128)(2,1)S(1)}, bf16[2,128,256]{2,1,0:T(8,128)(2,1)}, u32[]{:S(2)}) copy-start(bf16[2,128,256]{2,1,0:T(8,128)(2,1)} %constant.16.clone.spread) | copy-start | bytes 393220
  28.4 8.7 %copy-start.8 = (bf16[128,128]{1,0:T(8,128)(2,1)S(1)}, bf16[128,128]{1,0:T(8,128)(2,1)}, u32[]{:S(2)}) copy-start(bf16[128,128]{1,0:T(8,128)(2,1)} %constant.14.clone.eye_hbm.eye) | copy-start | bytes 98308
  29.8 7.3 %copy-start = (bf16[2,128,512]{2,1,0:T(8,128)(2,1)S(1)}, bf16[2,128,512]{2,1,0:T(8,128)(2,1)}, u32[]{:S(2)}) copy-start(bf16[2,128,512]{2,1,0:T(8,128)(2,1)} %in_w.1) | copy-start | bytes 786436
  29.8 20.2 %all-to-all-start.1 = ((bf16[256,2,128]{2,1,0:T(2,128)(2,1)}), bf16[256,2,128]{2,1,0:T(2,128)(2,1)S(1)}, u32[]{:S(2)}, u32[]{:S(2)}) async-start(bf16[256,2,128]{2,1,0:T(2,128)(2,1)} %bitcast.3), calls=%async_computation.1 | async-start | bytes 262144 | tf_op jit(solution)/shard_map/all_to_all | solution.py:229
  37.1 12.9 %copy-start.4 = (bf16[256,256]{1,0:T(8,128)(2,1)S(1)}, bf16[256,256]{1,0:T(8,128)(2,1)}, u32[]{:S(2)}) copy-start(bf16[256,256]{1,0:T(8,128)(2,1)} %constant.15.clone.deal_hbm.deal) | copy-start | bytes 393220
  50.0 13.8 %copy-start.3 = (bf16[2,512,256]{2,1,0:T(8,128)(2,1)S(1)}, bf16[2,512,256]{2,1,0:T(8,128)(2,1)}, u32[]{:S(2)}) copy-start(bf16[2,512,256]{2,1,0:T(8,128)(2,1)} %constant.20.clone.targets) | copy-start | bytes 1572868
  50.7 13.1 %copy-start.9 = (bf16[128,128]{1,0:T(8,128)(2,1)S(1)}, bf16[128,128]{1,0:T(8,128)(2,1)}, u32[]{:S(2)}) copy-start(bf16[128,128]{1,0:T(8,128)(2,1)} %constant.19.clone.take) | copy-start | bytes 98308
  65.3 21.5 %all-to-all-start.3 = ((bf16[256,4,128]{2,1,0:T(4,128)(2,1)}), bf16[256,4,128]{2,1,0:T(4,128)(2,1)S(1)}, u32[]{:S(2)}, u32[]{:S(2)}) async-start(bf16[256,4,128]{2,1,0:T(4,128)(2,1)} %bitcast.7), calls=%async_computation.3 | async-start | bytes 524288 | tf_op jit(solution)/shard_map/all_to_all | solution.py:229

commit v5 on v4

--- a/solution.py
+++ b/solution.py
@@ -51,7 +51,12 @@
 SPREAD = np.stack(
     [one_hot(256, 128, lambda i: i // 2, lambda i: i % 2 == r).T for r in range(2)]
 )
-EYE = one_hot(128, 128, lambda i: i)
+
+
+def identity():
+    row = lax.broadcasted_iota(jnp.int32, (128, 128), 0)
+    col = lax.broadcasted_iota(jnp.int32, (128, 128), 1)
+    return (row == col).astype(F32).astype(BF16)
 
 
 def normalized(values):
@@ -119,7 +124,7 @@
     gate_t = [transposed(gate_w[u], eye) for u in range(2)]
     out_t = [transposed(out_w[u], eye) for u in range(2)]
     spread_w = [jnp.concatenate([moved(t, spread[r]) for r in range(2)], 0) for t in out_t]
-    return gates(gate_t[0], state), transposed(in_w[1], eye), gate_t[1], *spread_w
+    return gates(gate_t[0], state), transposed(in_w, eye), gate_t[1], *spread_w
 
 
 def outgoing_math(received, sides, rows):
@@ -168,28 +173,35 @@
     return jnp.concatenate([nt(eye, refined[0:128]), nt(eye, refined[128:256])], 0).astype(BF16)
 
 
-def first_kernel(own_hbm, in_hbm, eye_hbm, deal_hbm, sent, state, own, in_w, eye, deal, done):
+def first_kernel(
+    own_hbm, in_hbm, deal_hbm, gate_hbm, out_hbm,
+    sent, state, next_in, gate_w, out_w, own, in_w, deal, done,
+):
+    routes = (
+        (own_hbm, own), (in_hbm.at[0], in_w), (deal_hbm, deal),
+        (in_hbm.at[1], next_in), (gate_hbm, gate_w), (out_hbm, out_w),
+    )
     copies = [
         pltpu.make_async_copy(source, target, done.at[k])
-        for k, (source, target) in enumerate(
-            ((own_hbm, own), (in_hbm.at[0], in_w), (eye_hbm, eye), (deal_hbm, deal))
-        )
+        for k, (source, target) in enumerate(routes)
     ]
     for copy in copies:
         copy.start()
-    for copy in copies:
+    for copy in copies[:3]:
         copy.wait()
-    sent[...], state[...] = first_math(own[...], in_w[...], eye[...], deal[...])
-
-
-def side_kernel(state, in_w, gate_w, out_w, eye, spread, gate, in_t, gate_t, spread_0, spread_1):
+    sent[...], state[...] = first_math(own[...], in_w[...], identity(), deal[...])
+    for copy in copies[3:]:
+        copy.wait()
+
+
+def outgoing_kernel(
+    received, state, in_w, gate_w, out_w, moves, sent, gate, in_t, gate_t, spread_0, spread_1
+):
+    sent[...] = outgoing_math(received[...], moves[0:256], moves[256:512])
     gate[...], in_t[...], gate_t[...], spread_0[...], spread_1[...] = side_math(
-        state[...], in_w[...], gate_w[...], out_w[...], eye[...], spread[...]
-    )
-
-
-def outgoing_kernel(received, sides, rows, sent):
-    sent[...] = outgoing_math(received[...], sides[...], rows[...])
+        state[...], in_w[...], gate_w[...], out_w[...], identity(),
+        (moves[512:640], moves[640:768]),
+    )
 
 
 def middle_kernel(gathered, state, gate, spread_w, in_t, deal, sent, middle):
@@ -198,16 +210,13 @@
     )
 
 
-def gate_kernel(gate_t, state, gate):
+def incoming_kernel(received, state, gate_t, take, targets, sent, gate):
+    sent[...] = incoming_math(received[...], take[...], targets[...])
     gate[...] = gates(gate_t[...], state[...])
 
 
-def incoming_kernel(received, take, targets, sent):
-    sent[...] = incoming_math(received[...], take[...], targets[...])
-
-
-def last_kernel(gathered, state, gate, spread_w, eye, refined):
-    refined[...] = last_math(gathered[...], state[...], gate[...], spread_w[...], eye[...])
+def last_kernel(gathered, state, gate, spread_w, refined):
+    refined[...] = last_math(gathered[...], state[...], gate[...], spread_w[...], identity())
 
 
 def call(kernel, outs, *arrays, space=pltpu.VMEM, scratch=()):
@@ -219,7 +228,6 @@
         out_specs=tuple(vmem for _ in outs),
         scratch_shapes=scratch,
         compiler_params=pltpu.CompilerParams(vmem_limit_bytes=16 << 20),
-        cost_estimate=pl.CostEstimate(flops=400_000_000, bytes_accessed=1 << 20, transcendentals=0),
     )(*arrays)
     return results if len(results) > 1 else results[0]
 
@@ -230,40 +238,37 @@
 
 
 def per_device(pair_rep, in_weights, gate_weights, out_weights):
-    eye, deal = jnp.asarray(EYE), jnp.asarray(DEAL)
+    deal = jnp.asarray(DEAL)
     kept = ((256, 128), F32)
     wide = ((256, 256), BF16)
-    inputs = [pair_rep.reshape(256, 128), in_weights, eye, deal]
-    sent, state = call(
-        first_kernel, [((512, 128), BF16), kept],
+    inputs = [pair_rep.reshape(256, 128), in_weights, deal, gate_weights, out_weights]
+    squares = ((2, 128, 128), BF16)
+    sent, state, next_in, gate_w, out_w = call(
+        first_kernel, [((512, 128), BF16), kept, ((128, 512), BF16), squares, squares],
         *(pltpu.with_memory_space_constraint(v, pltpu.HBM) for v in inputs),
         space=pltpu.HBM,
         scratch=[
             pltpu.VMEM((256, 128), BF16), pltpu.VMEM((128, 512), BF16),
-            pltpu.VMEM((128, 128), BF16), pltpu.VMEM((256, 256), BF16),
-            pltpu.SemaphoreType.DMA((4,)),
+            pltpu.VMEM((256, 256), BF16), pltpu.SemaphoreType.DMA((6,)),
         ],
     )
-    gate, in_t, gate_t, spread_0, spread_1 = call(
-        side_kernel, [kept, ((512, 128), BF16), ((128, 128), BF16), wide, wide],
-        state, in_weights, gate_weights, out_weights, eye, jnp.asarray(SPREAD),
-    )
-    sent = call(
-        outgoing_kernel, [((512, 128), BF16)],
-        exchanged(sent, CHIPS), jnp.asarray(SIDES), jnp.asarray(ROWS),
+    sent, gate, in_t, gate_t, spread_0, spread_1 = call(
+        outgoing_kernel,
+        [((512, 128), BF16), kept, ((512, 128), BF16), ((128, 128), BF16), wide, wide],
+        exchanged(sent, CHIPS), state, next_in, gate_w, out_w,
+        jnp.asarray(np.concatenate([SIDES, ROWS, *SPREAD], 0)),
     )
     sent, state = call(
         middle_kernel, [((512, 128), BF16), kept],
         exchanged(sent, TO_OWNERS), state, gate, spread_0, in_t, deal,
     )
-    gate = call(gate_kernel, [kept], gate_t, state)
-    sent = call(
-        incoming_kernel, [((1024, 128), BF16)],
-        exchanged(sent, LAYER), jnp.asarray(TAKE), jnp.asarray(TARGETS),
+    sent, gate = call(
+        incoming_kernel, [((1024, 128), BF16), kept],
+        exchanged(sent, LAYER), state, gate_t, jnp.asarray(TAKE), jnp.asarray(TARGETS),
     )
     refined = call(
         last_kernel, [((256, 128), BF16)],
-        exchanged(sent, FROM_LAYER), state, gate, spread_1, eye,
+        exchanged(sent, FROM_LAYER), state, gate, spread_1,
     )
     return refined.reshape(pair_rep.shape)
 

time: 88.1 us -> 86.3 us (0.980)
  blocking collectives: 39.6 us -> 80.6 us
  waiting for transfers between devices: 27.9 us -> 0 us
  starting transfers between devices: 12.9 us -> 0 us
  Pallas kernels: 7.17 us -> 5.33 us
    all_to_all x2 -> x4, blocking collectives: 39.6 us -> 80.6 us  [exchanged(): return lax.all_to_all(blocks, axes, 0, 0, tiled=True).reshape(rows.shape)]
    all_to_all x2 -> x0, waiting for transfers between devices: 27.9 us -> none  [exchanged(): return lax.all_to_all(blocks, axes, 0, 0, tiled=True).reshape(rows.shape)]
    all_to_all x2 -> x0, starting transfers between devices: 12.9 us -> none  [exchanged(): return lax.all_to_all(blocks, axes, 0, 0, tiled=True).reshape(rows.shape)]
    pallas_call x7 -> x5, Pallas kernels: 7.17 us -> 5.33 us  [call(): pl.pallas_call(kernel, out_shape=tuple((jax.ShapeDtypeStruct(shape, dtype...]
  transfers between devices with their start and end apart: 2 -> 0, of which waited for: 2 -> 0; matrix products, arithmetic and copies ran while one was open for 0% -> 0% of each run, Pallas kernels for 1% -> 0%
where the time goes in v5:
time: 86.3 us; the launch traced here: 86 us
  blocking collectives  80.6 us (93%)
  Pallas kernels  5.33 us (6%)
    all_to_all x4, blocking collectives, exchanged(): return lax.all_to_all(blocks, axes, 0, 0, tiled=True).reshape(rows.shape)  80.6 us
    pallas_call x5, Pallas kernels, call(): pl.pallas_call(kernel, out_shape=tuple((jax.ShapeDtypeStruct(shape, dtype...  5.33 us

profile of v5, /device:TPU:1, one launch (start us, length us, event | category | flops | bytes accessed | tf_op | source)
XLA Modules:
  0.0 86.0 jit_solution(13971763012565485326)
XLA Ops:
  0.0 0.0 copy-start.2
  0.0 1.8 %shard_map.82 = (bf16[512,128]{1,0:T(8,128)(2,1)S(1)}, f32[256,128]{1,0:T(8,128)S(1)}, bf16[128,512]{1,0:T(8,128)(2,1)S(1)}, bf16[2,128,128]{2,1,0:T(8,128)(2,1)S(1)}, bf16[2,128,128]{2,1,0:T(8,128)(2,1)S(1)}) custom-call(bf16[256,128]{1,0:T(8,128)(2,1)} %bitcast.18, bf16[2,128,512]{2,1,0:T(8,128)(2,1)} %in_hbm.1, ...), custom_call_target="tpu_custom_call" | custom-call | tf_op jit(solution)/shard_map/pallas_call | solution.py:224
  1.8 26.5 %all_to_all.20 = bf16[128,4,128]{2,1,0:T(4,128)(2,1)S(1)} all-to-all(bf16[128,4,128]{2,1,0:T(4,128)(2,1)S(1)} %bitcast.17), channel_id=1, replica_groups=mesh['y'=4,'x'=4,'zh'=4,'zl'=2,'c'=2] {'zl','y','x','zh'}, dimensions={0} | all-to-all | bytes 262144 | tf_op jit(solution)/shard_map/all_to_all | solution.py:237
  28.2 0.0 copy-done.2
  28.2 1.0 %shard_map.83 = (bf16[512,128]{1,0:T(8,128)(2,1)S(1)}, f32[256,128]{1,0:T(8,128)S(1)}, bf16[512,128]{1,0:T(8,128)(2,1)S(1)}, bf16[128,128]{1,0:T(8,128)(2,1)S(1)...) custom-call(bf16[512,128]{1,0:T(8,128)(2,1)S(1)} %bitcast.11, f32[256,128]{1,0:T(8,128)S(1)} %get-tuple-element.21.state, ...), custom_call_target="tpu_custom_call" | custom-call | tf_op jit(solution)/shard_map/pallas_call | solution.py:224
  29.2 0.0 copy-start.1
  29.2 19.9 %all_to_all.21 = bf16[256,2,128]{2,1,0:T(2,128)(2,1)S(1)} all-to-all(bf16[256,2,128]{2,1,0:T(2,128)(2,1)S(1)} %bitcast.15), channel_id=1, replica_groups=mesh['y'=4,'x'=4,'zh'=4,'zl'=2,'c'=2] {'zl','c','y','x','zh'}, dimensions={0} | all-to-all | bytes 262144 | tf_op jit(solution)/shard_map/all_to_all | solution.py:237
  49.1 0.0 copy-done.1
  49.1 0.0 copy-start
  49.1 0.7 shard_map.84
  49.9 0.0 copy-start.3
  49.9 13.1 %all_to_all.22 = bf16[64,8,128]{2,1,0:T(8,128)(2,1)S(1)} all-to-all(bf16[64,8,128]{2,1,0:T(8,128)(2,1)S(1)} %bitcast.16), channel_id=1, replica_groups=mesh['y'=4,'x'=4,'zh'=4,'zl'=2,'c'=2] {'zl','c','y','x'}, dimensions={0} | all-to-all | bytes 262144 | tf_op jit(solution)/shard_map/all_to_all | solution.py:237
  63.0 0.0 copy-done
  63.0 0.0 copy-done.3
  63.0 0.8 shard_map.85
  63.8 21.2 %all_to_all.23 = bf16[256,4,128]{2,1,0:T(4,128)(2,1)S(1)} all-to-all(bf16[256,4,128]{2,1,0:T(4,128)(2,1)S(1)} %bitcast.14), channel_id=1, replica_groups=mesh['y'=4,'x'=4,'zh'=4,'zl'=2,'c'=2] {'zh','zl','c','y','x'}, dimensions={0} | all-to-all | bytes 524288 | tf_op jit(solution)/shard_map/all_to_all | solution.py:237
  85.0 1.1 %shard_map.86 = bf16[256,128]{1,0:T(8,128)(2,1)} custom-call(bf16[1024,128]{1,0:T(8,128)(2,1)S(1)} %bitcast.10, f32[256,128]{1,0:T(8,128)S(1)} %get-tuple-element.30.state, f32[256,128]{1,0:T(8,128)S(1)} %get-tuple-element.33.gate, bf16[256,256]{1,0:T(8,128)(2,1)S(1)} %get-tuple-element.34.spread_w), custom_call_target="tpu_custom_call" | custom-call | tf_op jit(solution)/shard_map/pallas_call | solution.py:224
Async XLA Ops:
  0.0 28.2 %copy-start.2 = (bf16[768,256]{1,0:T(8,128)(2,1)S(1)}, bf16[768,256]{1,0:T(8,128)(2,1)}, u32[]{:S(2)}) copy-start(bf16[768,256]{1,0:T(8,128)(2,1)} %constant.9.clone.moves) | copy-start | bytes 1179652
  29.2 19.9 %copy-start.1 = (bf16[256,256]{1,0:T(8,128)(2,1)S(1)}, bf16[256,256]{1,0:T(8,128)(2,1)}, u32[]{:S(2)}) copy-start(bf16[256,256]{1,0:T(8,128)(2,1)} %constant.8.clone.deal_hbm.deal) | copy-start | bytes 393220
  49.1 13.8 %copy-start = (bf16[2,512,256]{2,1,0:T(8,128)(2,1)S(1)}, bf16[2,512,256]{2,1,0:T(8,128)(2,1)}, u32[]{:S(2)}) copy-start(bf16[2,512,256]{2,1,0:T(8,128)(2,1)} %constant.11.clone.targets) | copy-start | bytes 1572868
  49.9 13.1 %copy-start.3 = (bf16[128,128]{1,0:T(8,128)(2,1)S(1)}, bf16[128,128]{1,0:T(8,128)(2,1)}, u32[]{:S(2)}) copy-start(bf16[128,128]{1,0:T(8,128)(2,1)} %constant.10.clone.take) | copy-start | bytes 98308

commit v6 on v5

--- a/solution.py
+++ b/solution.py
@@ -12,8 +12,8 @@
 
 CHIPS = ("zl", "y", "x", "zh")
 TO_OWNERS = ("zl", "c", "y", "x", "zh")
-LAYER = ("zl", "c", "y", "x")
-FROM_LAYER = ("zh", "zl", "c", "y", "x")
+LAYER = ("c", "zl", "y", "x")
+FROM_LAYER = ("zh", "zl", "y", "x")
 
 
 def nn(a, b):
@@ -26,6 +26,10 @@
 
 def moved(one_hot, values):
     return nn(one_hot, values).astype(BF16)
+
+
+def moved_t(one_hot, values):
+    return nt(one_hot, values).astype(BF16)
 
 
 def one_hot(rows, cols, source, valid=lambda i: i >= 0):
@@ -37,17 +41,19 @@
 DEAL = one_hot(256, 256, lambda i: i % 4 * 64 + i // 4)
 SIDES = one_hot(256, 256, lambda i: i % 128 // 2 * 4 + i // 128 * 2 + i % 2)
 ROWS = one_hot(256, 256, lambda i: i % 2 * 128 + i // 2)
-TAKE = one_hot(128, 128, lambda i: i % 16 * 8 + i // 16)
-TARGETS = np.stack(
+TAKE = np.concatenate(
     [
         one_hot(
-            512, 256,
-            lambda i: i % 64 // 4 * 16 + i % 256 // 64 * 4 + i % 2 * 2 + i // 256,
-            lambda i: i // 2 % 2 == channel,
+            128, 256,
+            lambda i: i % 16 * 16 + i // 32 * 4 + side * 2 + i // 16 % 2,
         )
-        for channel in range(2)
+        for side in range(2)
     ]
 )
+TARGETS = one_hot(
+    256, 256, lambda i: i % 32 // 2 * 16 + i % 128 // 32 * 4 + i % 2 * 2 + i // 128
+)
+MIX = one_hot(128, 128, lambda i: i % 8 // 2 * 32 + i // 8 * 2 + i % 2)
 SPREAD = np.stack(
     [one_hot(256, 128, lambda i: i // 2, lambda i: i % 2 == r).T for r in range(2)]
 )
@@ -115,16 +121,28 @@
     return (state + gate * update).astype(BF16)
 
 
-def first_math(own, in_w, eye, deal):
+def first_math(own, in_w, deal):
+    values = own.astype(F32)
+    shifted = values - jnp.mean(values, axis=1, keepdims=True)
+    spread = jnp.mean(shifted * shifted, axis=1, keepdims=True)
+    normed = (shifted * lax.rsqrt(spread + EPSILON)).astype(BF16)
+    projected = nn(normed, in_w)
+    blocks = ([], [])
+    for k in (0, 256):
+        product = sigmoid(projected[:, k : k + 128]) * projected[:, k + 128 : k + 256]
+        for block, half in zip(blocks, halves_swapped(product[0:128], product[128:256])):
+            block.append(half)
+    return jnp.concatenate(
+        [moved_t(deal, jnp.concatenate(b, 1).astype(BF16)) for b in blocks], 0
+    )
+
+
+def side_math(own, in_w, gate_w, out_w, eye, spread):
     state = jnp.concatenate([nt(eye, own[0:128]), nt(eye, own[128:256])], 0)
-    return sent_operands(transposed(in_w, eye), normalized(state), deal), state
-
-
-def side_math(state, in_w, gate_w, out_w, eye, spread):
     gate_t = [transposed(gate_w[u], eye) for u in range(2)]
     out_t = [transposed(out_w[u], eye) for u in range(2)]
     spread_w = [jnp.concatenate([moved(t, spread[r]) for r in range(2)], 0) for t in out_t]
-    return gates(gate_t[0], state), transposed(in_w, eye), gate_t[1], *spread_w
+    return state, gates(gate_t[0], state), transposed(in_w, eye), gate_t[1], *spread_w
 
 
 def outgoing_math(received, sides, rows):
@@ -143,28 +161,30 @@
     parts = gathered.astype(F32).reshape(2, 2, 128, 128)
     product = (parts[:, 0] + parts[:, 1]).reshape(256, 128)
     middle = residual(product, spread_w, state, gate).astype(F32)
-    return sent_operands(in_t, normalized(middle), deal), middle
-
-
-def incoming_math(received, take, targets):
-    blocks = [nn(take, received[128 * ka : 128 * ka + 128]) for ka in range(4)]
-    swapped = [halves_swapped(blocks[0], blocks[1]), halves_swapped(blocks[2], blocks[3])]
-
-    def side_of(place):
-        rows = slice(32 * place, 32 * place + 32)
-        return jnp.concatenate(
-            [jnp.concatenate([half[rows] for half in pair], 0) for pair in swapped], 1
-        ).astype(BF16)
-
-    lefts = [nt(targets[channel], side_of(2 * channel)).astype(BF16) for channel in range(2)]
-    right = jnp.concatenate([side_of(1), side_of(3)], 0)
-    total = nn(jnp.concatenate(lefts, 1), right)
-    blocks = []
-    for k in (0, 128):
-        blocks.extend(halves_swapped(total[0:256, k : k + 128], total[256:512, k : k + 128]))
-    return jnp.concatenate(
-        [b[64 * zh : 64 * zh + 64] for zh in range(4) for b in blocks], 0
-    ).astype(BF16)
+    sent = sent_operands(in_t, normalized(middle), deal)
+    return jnp.concatenate([sent, sent], 0), middle
+
+
+def incoming_math(received, own_core, take, targets, mix):
+    blocks = [nn(take[0:128], received[256 * k : 256 * k + 256]) for k in range(4)]
+    lefts = [halves_swapped(blocks[zl], blocks[zl + 2]) for zl in range(2)]
+    blocks = [nn(take[128:256], own_core[256 * zl : 256 * zl + 256]) for zl in range(2)]
+    rights = halves_swapped(*blocks)
+    totals = []
+    for channel in range(4):
+        rows = slice(32 * channel, 32 * channel + 32)
+        left = jnp.concatenate(
+            [jnp.concatenate([half[rows] for half in pair], 0) for pair in lefts], 1
+        )
+        right = jnp.concatenate([half[rows] for half in rights], 0)
+        total = nn(moved_t(targets, left.astype(BF16)), right.astype(BF16))
+        totals.append([v.astype(BF16) for v in halves_swapped(total[0:128], total[128:256])])
+    sent = []
+    for zh in range(4):
+        rows = slice(32 * zh, 32 * zh + 32)
+        for zl in range(2):
+            sent.append(moved(mix, jnp.concatenate([pair[zl][rows] for pair in totals], 0)))
+    return jnp.concatenate(sent, 0)
 
 
 def last_math(gathered, state, gate, spread_w, eye):
@@ -175,7 +195,7 @@
 
 def first_kernel(
     own_hbm, in_hbm, deal_hbm, gate_hbm, out_hbm,
-    sent, state, next_in, gate_w, out_w, own, in_w, deal, done,
+    sent, own, next_in, gate_w, out_w, in_w, deal, done,
 ):
     routes = (
         (own_hbm, own), (in_hbm.at[0], in_w), (deal_hbm, deal),
@@ -189,17 +209,18 @@
         copy.start()
     for copy in copies[:3]:
         copy.wait()
-    sent[...], state[...] = first_math(own[...], in_w[...], identity(), deal[...])
+    sent[...] = first_math(own[...], in_w[...], deal[...])
     for copy in copies[3:]:
         copy.wait()
 
 
 def outgoing_kernel(
-    received, state, in_w, gate_w, out_w, moves, sent, gate, in_t, gate_t, spread_0, spread_1
+    received, own, in_w, gate_w, out_w, moves,
+    sent, state, gate, in_t, gate_t, spread_0, spread_1,
 ):
     sent[...] = outgoing_math(received[...], moves[0:256], moves[256:512])
-    gate[...], in_t[...], gate_t[...], spread_0[...], spread_1[...] = side_math(
-        state[...], in_w[...], gate_w[...], out_w[...], identity(),
+    state[...], gate[...], in_t[...], gate_t[...], spread_0[...], spread_1[...] = side_math(
+        own[...], in_w[...], gate_w[...], out_w[...], identity(),
         (moves[512:640], moves[640:768]),
     )
 
@@ -210,8 +231,9 @@
     )
 
 
-def incoming_kernel(received, state, gate_t, take, targets, sent, gate):
-    sent[...] = incoming_math(received[...], take[...], targets[...])
+def incoming_kernel(received, state, gate_t, moves, mix, sent, gate):
+    own_core = received[pl.ds(pl.multiple_of(lax.axis_index("c") * 512, 512), 512)]
+    sent[...] = incoming_math(received[...], own_core, moves[0:256], moves[256:512], mix[...])
     gate[...] = gates(gate_t[...], state[...])
 
 
@@ -242,29 +264,30 @@
     kept = ((256, 128), F32)
     wide = ((256, 256), BF16)
     inputs = [pair_rep.reshape(256, 128), in_weights, deal, gate_weights, out_weights]
-    squares = ((2, 128, 128), BF16)
-    sent, state, next_in, gate_w, out_w = call(
-        first_kernel, [((512, 128), BF16), kept, ((128, 512), BF16), squares, squares],
+    block, weights, square = ((256, 128), BF16), ((128, 512), BF16), ((2, 128, 128), BF16)
+    sent, own, next_in, gate_w, out_w = call(
+        first_kernel, [((512, 128), BF16), block, weights, square, square],
         *(pltpu.with_memory_space_constraint(v, pltpu.HBM) for v in inputs),
         space=pltpu.HBM,
         scratch=[
-            pltpu.VMEM((256, 128), BF16), pltpu.VMEM((128, 512), BF16),
-            pltpu.VMEM((256, 256), BF16), pltpu.SemaphoreType.DMA((6,)),
+            pltpu.VMEM((128, 512), BF16), pltpu.VMEM((256, 256), BF16),
+            pltpu.SemaphoreType.DMA((6,)),
         ],
     )
-    sent, gate, in_t, gate_t, spread_0, spread_1 = call(
+    sent, state, gate, in_t, gate_t, spread_0, spread_1 = call(
         outgoing_kernel,
-        [((512, 128), BF16), kept, ((512, 128), BF16), ((128, 128), BF16), wide, wide],
-        exchanged(sent, CHIPS), state, next_in, gate_w, out_w,
+        [((512, 128), BF16), kept, kept, ((512, 128), BF16), ((128, 128), BF16), wide, wide],
+        exchanged(sent, CHIPS), own, next_in, gate_w, out_w,
         jnp.asarray(np.concatenate([SIDES, ROWS, *SPREAD], 0)),
     )
     sent, state = call(
-        middle_kernel, [((512, 128), BF16), kept],
+        middle_kernel, [((1024, 128), BF16), kept],
         exchanged(sent, TO_OWNERS), state, gate, spread_0, in_t, deal,
     )
     sent, gate = call(
         incoming_kernel, [((1024, 128), BF16), kept],
-        exchanged(sent, LAYER), state, gate_t, jnp.asarray(TAKE), jnp.asarray(TARGETS),
+        exchanged(sent, LAYER), state, gate_t,
+        jnp.asarray(np.concatenate([TAKE, TARGETS], 0)), jnp.asarray(MIX),
     )
     refined = call(
         last_kernel, [((256, 128), BF16)],

time: 86.3 us -> 86.6 us (level)
  no operation moved by 1% of the time
where the time goes in v6:
time: 86.6 us; the launch traced here: 86.2 us
  blocking collectives  80.1 us (92%)
  Pallas kernels  5.98 us (7%)
    all_to_all x4, blocking collectives, exchanged(): return lax.all_to_all(blocks, axes, 0, 0, tiled=True).reshape(rows.shape)  80.1 us
    pallas_call x5, Pallas kernels, call(): pl.pallas_call(kernel, out_shape=tuple((jax.ShapeDtypeStruct(shape, dtype...  5.98 us

profile of v6, /device:TPU:1, one launch (start us, length us, event | category | flops | bytes accessed | tf_op | source)
XLA Modules:
  0.0 86.2 jit_solution(5580693541606465714)
XLA Ops:
  0.0 0.0 copy-start.1
  0.0 1.8 %shard_map.82 = (bf16[512,128]{1,0:T(8,128)(2,1)S(1)}, bf16[256,128]{1,0:T(8,128)(2,1)S(1)}, bf16[128,512]{1,0:T(8,128)(2,1)S(1)}, bf16[2,128,128]{2,1,0:T(8,128)(2,1)S(1)}, bf16[2,128,128]{2,1,0:T(8,128)(2,1)S(1)}) custom-call(bf16[256,128]{1,0:T(8,128)(2,1)} %bitcast.18, bf16[2,128,512]{2,1,0:T(8,128)(2,1)} %in_hbm.1, ...), custom_call_target="tpu_custom_call" | custom-call | tf_op jit(solution)/shard_map/pallas_call | solution.py:246
  1.8 26.5 %all_to_all.20 = bf16[128,4,128]{2,1,0:T(4,128)(2,1)S(1)} all-to-all(bf16[128,4,128]{2,1,0:T(4,128)(2,1)S(1)} %bitcast.17), channel_id=1, replica_groups=mesh['y'=4,'x'=4,'zh'=4,'zl'=2,'c'=2] {'zl','y','x','zh'}, dimensions={0} | all-to-all | bytes 262144 | tf_op jit(solution)/shard_map/all_to_all | solution.py:259
  28.3 0.0 copy-done.1
  28.3 1.0 %shard_map.83 = (bf16[512,128]{1,0:T(8,128)(2,1)S(1)}, f32[256,128]{1,0:T(8,128)S(1)}, f32[256,128]{1,0:T(8,128)S(1)}, bf16[512,128]{1,0:T(8,128)(2,1)S(1)}, bf1...) custom-call(bf16[512,128]{1,0:T(8,128)(2,1)S(1)} %bitcast.12, ...), custom_call_target="tpu_custom_call" | custom-call | tf_op jit(solution)/shard_map/pallas_call | solution.py:246
  29.3 0.0 copy-start
  29.3 19.9 %all_to_all.21 = bf16[256,2,128]{2,1,0:T(2,128)(2,1)S(1)} all-to-all(bf16[256,2,128]{2,1,0:T(2,128)(2,1)S(1)} %bitcast.16), channel_id=1, replica_groups=mesh['y'=4,'x'=4,'zh'=4,'zl'=2,'c'=2] {'zl','c','y','x','zh'}, dimensions={0} | all-to-all | bytes 262144 | tf_op jit(solution)/shard_map/all_to_all | solution.py:259
  49.2 0.0 copy-done
  49.2 0.7 shard_map.84
  49.9 0.0 copy-start.2
  50.0 0.0 copy-start.3
  50.0 14.8 %all_to_all.22 = bf16[64,16,128]{2,1,0:T(8,128)(2,1)S(1)} all-to-all(bf16[64,16,128]{2,1,0:T(8,128)(2,1)S(1)} %bitcast.14), channel_id=1, replica_groups=mesh['y'=4,'x'=4,'zh'=4,'zl'=2,'c'=2] {'c','zl','y','x'}, dimensions={0} | all-to-all | bytes 524288 | tf_op jit(solution)/shard_map/all_to_all | solution.py:259
  64.7 0.0 copy-done.2
  64.7 0.0 copy-done.3
  64.8 1.4 %shard_map.85 = (bf16[1024,128]{1,0:T(8,128)(2,1)S(1)}, f32[256,128]{1,0:T(8,128)S(1)}) custom-call(bf16[1024,128]{1,0:T(8,128)(2,1)S(1)} %bitcast.10, f32[256,128]{1,0:T(8,128)S(1)} %get-tuple-element.32.state, bf16[128,128]{1,0:T(8,128)(2,1)S(1)} %get-tuple-element.33.gate_t, bf16[512,256]{1,0:T(8,128)(2,1)S(1)} %copy-done.2, bf16[128,128]{1,0:T(8,128)(2,1)S(1)} %copy-done.3), custom_call_target="tpu_custom_call" | custom-call | tf_op jit(solution)/shard_map/pallas_call | solution.py:246
  66.2 18.9 %all_to_all.23 = bf16[128,8,128]{2,1,0:T(8,128)(2,1)S(1)} all-to-all(bf16[128,8,128]{2,1,0:T(8,128)(2,1)S(1)} %bitcast.15), channel_id=1, replica_groups=mesh['y'=4,'x'=4,'zh'=4,'zl'=2,'c'=2] {'zh','zl','y','x'}, dimensions={0} | all-to-all | bytes 524288 | tf_op jit(solution)/shard_map/all_to_all | solution.py:259
  85.1 1.1 %shard_map.86 = bf16[256,128]{1,0:T(8,128)(2,1)} custom-call(bf16[1024,128]{1,0:T(8,128)(2,1)S(1)} %bitcast.11, f32[256,128]{1,0:T(8,128)S(1)} %get-tuple-element.32.state, f32[256,128]{1,0:T(8,128)S(1)} %get-tuple-element.35.gate, bf16[256,256]{1,0:T(8,128)(2,1)S(1)} %get-tuple-element.36.spread_w), custom_call_target="tpu_custom_call" | custom-call | tf_op jit(solution)/shard_map/pallas_call | solution.py:246
Async XLA Ops:
  0.0 28.3 %copy-start.1 = (bf16[768,256]{1,0:T(8,128)(2,1)S(1)}, bf16[768,256]{1,0:T(8,128)(2,1)}, u32[]{:S(2)}) copy-start(bf16[768,256]{1,0:T(8,128)(2,1)} %constant.9.clone.moves) | copy-start | bytes 1179652
  29.3 19.9 %copy-start = (bf16[256,256]{1,0:T(8,128)(2,1)S(1)}, bf16[256,256]{1,0:T(8,128)(2,1)}, u32[]{:S(2)}) copy-start(bf16[256,256]{1,0:T(8,128)(2,1)} %constant.8.clone.deal_hbm.deal) | copy-start | bytes 393220
  49.9 14.8 %copy-start.2 = (bf16[512,256]{1,0:T(8,128)(2,1)S(1)}, bf16[512,256]{1,0:T(8,128)(2,1)}, u32[]{:S(2)}) copy-start(bf16[512,256]{1,0:T(8,128)(2,1)} %constant.10.clone.moves) | copy-start | bytes 786436
  50.0 14.8 %copy-start.3 = (bf16[128,128]{1,0:T(8,128)(2,1)S(1)}, bf16[128,128]{1,0:T(8,128)(2,1)}, u32[]{:S(2)}) copy-start(bf16[128,128]{1,0:T(8,128)(2,1)} %constant.11.clone.mix) | copy-start | bytes 98308

commit v7 on v5

--- a/solution.py
+++ b/solution.py
@@ -10,10 +10,9 @@
 BF16 = jnp.bfloat16
 F32 = jnp.float32
 
-CHIPS = ("zl", "y", "x", "zh")
-TO_OWNERS = ("zl", "c", "y", "x", "zh")
+CHIPS = ("zh", "zl", "y", "x")
 LAYER = ("zl", "c", "y", "x")
-FROM_LAYER = ("zh", "zl", "c", "y", "x")
+ALL = ("zh", "zl", "c", "y", "x")
 
 
 def nn(a, b):
@@ -36,7 +35,9 @@
 
 DEAL = one_hot(256, 256, lambda i: i % 4 * 64 + i // 4)
 SIDES = one_hot(256, 256, lambda i: i % 128 // 2 * 4 + i // 128 * 2 + i % 2)
-ROWS = one_hot(256, 256, lambda i: i % 2 * 128 + i // 2)
+ROWS = one_hot(
+    256, 256, lambda i: i % 2 * 128 + i % 16 // 4 * 32 + i // 16 * 2 + i % 4 // 2
+)
 TAKE = one_hot(128, 128, lambda i: i % 16 * 8 + i // 16)
 TARGETS = np.stack(
     [
@@ -128,7 +129,10 @@
 
 
 def outgoing_math(received, sides, rows):
-    split = [nn(sides, received[256 * zl : 256 * zl + 256]) for zl in range(2)]
+    split = []
+    for zl in range(2):
+        starts = range(64 * zl, 512, 128)
+        split.append(nn(sides, jnp.concatenate([received[k : k + 64] for k in starts], 0)))
     left = [v.astype(BF16) for v in halves_swapped(split[0][0:128], split[1][0:128])]
     right = jnp.concatenate(halves_swapped(split[0][128:256], split[1][128:256]), 0)
     right = moved(rows, right.astype(BF16))
@@ -136,11 +140,13 @@
     blocks = []
     for k in (0, 128):
         blocks.extend(halves_swapped(even[:, k : k + 128], odd[:, k : k + 128]))
-    return jnp.concatenate(blocks, 0).astype(BF16)
+    return jnp.concatenate(
+        [b[32 * zh : 32 * zh + 32] for zh in range(4) for b in blocks], 0
+    ).astype(BF16)
 
 
 def middle_math(gathered, state, gate, spread_w, in_t, deal):
-    parts = gathered.astype(F32).reshape(2, 2, 128, 128)
+    parts = gathered.astype(F32).reshape(8, 2, 32, 128)
     product = (parts[:, 0] + parts[:, 1]).reshape(256, 128)
     middle = residual(product, spread_w, state, gate).astype(F32)
     return sent_operands(in_t, normalized(middle), deal), middle
@@ -174,23 +180,28 @@
 
 
 def first_kernel(
-    own_hbm, in_hbm, deal_hbm, gate_hbm, out_hbm,
-    sent, state, next_in, gate_w, out_w, own, in_w, deal, done,
+    own_hbm, in_hbm, gate_hbm, out_hbm, moves_hbm,
+    sent, state, next_in, gate_w, out_w, moves, own, in_w, done,
 ):
     routes = (
-        (own_hbm, own), (in_hbm.at[0], in_w), (deal_hbm, deal),
-        (in_hbm.at[1], next_in), (gate_hbm, gate_w), (out_hbm, out_w),
+        (own_hbm, own), (in_hbm.at[0], in_w), (in_hbm.at[1], next_in),
+        (gate_hbm, gate_w), (out_hbm, out_w), (moves_hbm, moves),
     )
     copies = [
         pltpu.make_async_copy(source, target, done.at[k])
         for k, (source, target) in enumerate(routes)
     ]
-    for copy in copies:
+    for copy in copies[:2]:
         copy.start()
-    for copy in copies[:3]:
+    row = lax.broadcasted_iota(jnp.int32, (256, 256), 0)
+    col = lax.broadcasted_iota(jnp.int32, (256, 256), 1)
+    deal = (col == row % 4 * 64 + row // 4).astype(F32).astype(BF16)
+    for copy in copies[:2]:
         copy.wait()
-    sent[...], state[...] = first_math(own[...], in_w[...], identity(), deal[...])
-    for copy in copies[3:]:
+    for copy in copies[2:]:
+        copy.start()
+    sent[...], state[...] = first_math(own[...], in_w[...], identity(), deal)
+    for copy in copies[2:]:
         copy.wait()
 
 
@@ -241,26 +252,27 @@
     deal = jnp.asarray(DEAL)
     kept = ((256, 128), F32)
     wide = ((256, 256), BF16)
-    inputs = [pair_rep.reshape(256, 128), in_weights, deal, gate_weights, out_weights]
+    moves = jnp.asarray(np.concatenate([SIDES, ROWS, *SPREAD], 0))
+    inputs = [pair_rep.reshape(256, 128), in_weights, gate_weights, out_weights, moves]
     squares = ((2, 128, 128), BF16)
-    sent, state, next_in, gate_w, out_w = call(
-        first_kernel, [((512, 128), BF16), kept, ((128, 512), BF16), squares, squares],
+    sent, state, next_in, gate_w, out_w, moves = call(
+        first_kernel,
+        [((512, 128), BF16), kept, ((128, 512), BF16), squares, squares, (moves.shape, BF16)],
         *(pltpu.with_memory_space_constraint(v, pltpu.HBM) for v in inputs),
         space=pltpu.HBM,
         scratch=[
             pltpu.VMEM((256, 128), BF16), pltpu.VMEM((128, 512), BF16),
-            pltpu.VMEM((256, 256), BF16), pltpu.SemaphoreType.DMA((6,)),
+            pltpu.SemaphoreType.DMA((6,)),
         ],
     )
     sent, gate, in_t, gate_t, spread_0, spread_1 = call(
         outgoing_kernel,
         [((512, 128), BF16), kept, ((512, 128), BF16), ((128, 128), BF16), wide, wide],
-        exchanged(sent, CHIPS), state, next_in, gate_w, out_w,
-        jnp.asarray(np.concatenate([SIDES, ROWS, *SPREAD], 0)),
+        exchanged(sent, CHIPS), state, next_in, gate_w, out_w, moves,
     )
     sent, state = call(
         middle_kernel, [((512, 128), BF16), kept],
-        exchanged(sent, TO_OWNERS), state, gate, spread_0, in_t, deal,
+        exchanged(sent, ALL), state, gate, spread_0, in_t, deal,
     )
     sent, gate = call(
         incoming_kernel, [((1024, 128), BF16), kept],
@@ -268,7 +280,7 @@
     )
     refined = call(
         last_kernel, [((256, 128), BF16)],
-        exchanged(sent, FROM_LAYER), state, gate, spread_1,
+        exchanged(sent, ALL), state, gate, spread_1,
     )
     return refined.reshape(pair_rep.shape)
 

time: 86.3 us -> 87.4 us (1.013)
  no operation moved by 1% of the time
where the time goes in v7:
time: 87.4 us; the launch traced here: 87.1 us
  blocking collectives  81.3 us (93%)
  Pallas kernels  5.7 us (7%)
    all_to_all x4, blocking collectives, exchanged(): return lax.all_to_all(blocks, axes, 0, 0, tiled=True).reshape(rows.shape)  81.3 us
    pallas_call x5, Pallas kernels, call(): pl.pallas_call(kernel, out_shape=tuple((jax.ShapeDtypeStruct(shape, dtype...  5.7 us

profile of v7, /device:TPU:1, one launch (start us, length us, event | category | flops | bytes accessed | tf_op | source)
XLA Modules:
  0.0 87.1 jit_solution(6595492585324234291)
XLA Ops:
  0.0 2.1 %shard_map.82 = (bf16[512,128]{1,0:T(8,128)(2,1)S(1)}, f32[256,128]{1,0:T(8,128)S(1)}, bf16[128,512]{1,0:T(8,128)(2,1)S(1)}, bf16[2,128,128]{2,1,0:T(8,128)(2,1)...) custom-call(bf16[256,128]{1,0:T(8,128)(2,1)} %bitcast.18, bf16[2,128,512]{2,1,0:T(8,128)(2,1)} %in_hbm.1, ...), custom_call_target="tpu_custom_call" | custom-call | tf_op jit(solution)/shard_map/pallas_call | solution.py:235
  2.1 27.4 %all_to_all.20 = bf16[128,4,128]{2,1,0:T(4,128)(2,1)S(1)} all-to-all(bf16[128,4,128]{2,1,0:T(4,128)(2,1)S(1)} %bitcast.17), channel_id=1, replica_groups=mesh['y'=4,'x'=4,'zh'=4,'zl'=2,'c'=2] {'zh','zl','y','x'}, dimensions={0} | all-to-all | bytes 262144 | tf_op jit(solution)/shard_map/all_to_all | solution.py:248
  29.5 1.0 %shard_map.83 = (bf16[512,128]{1,0:T(8,128)(2,1)S(1)}, f32[256,128]{1,0:T(8,128)S(1)}, bf16[512,128]{1,0:T(8,128)(2,1)S(1)}, bf16[128,128]{1,0:T(8,128)(2,1)S(1)...) custom-call(bf16[512,128]{1,0:T(8,128)(2,1)S(1)} %bitcast.11, f32[256,128]{1,0:T(8,128)S(1)} %get-tuple-element.22.state, ...), custom_call_target="tpu_custom_call" | custom-call | tf_op jit(solution)/shard_map/pallas_call | solution.py:235
  30.5 0.0 copy-start.1
  30.5 20.2 %all_to_all.21 = bf16[256,2,128]{2,1,0:T(2,128)(2,1)S(1)} all-to-all(bf16[256,2,128]{2,1,0:T(2,128)(2,1)S(1)} %bitcast.15), channel_id=1, replica_groups=mesh['y'=4,'x'=4,'zh'=4,'zl'=2,'c'=2] {'zh','zl','c','y','x'}, dimensions={0} | all-to-all | bytes 262144 | tf_op jit(solution)/shard_map/all_to_all | solution.py:248
  50.6 0.0 copy-done.1
  50.6 0.0 copy-start
  50.7 0.7 shard_map.84
  51.4 0.0 copy-start.2
  51.4 12.6 %all_to_all.22 = bf16[64,8,128]{2,1,0:T(8,128)(2,1)S(1)} all-to-all(bf16[64,8,128]{2,1,0:T(8,128)(2,1)S(1)} %bitcast.16), channel_id=1, replica_groups=mesh['y'=4,'x'=4,'zh'=4,'zl'=2,'c'=2] {'zl','c','y','x'}, dimensions={0} | all-to-all | bytes 262144 | tf_op jit(solution)/shard_map/all_to_all | solution.py:248
  64.0 0.0 copy-done
  64.0 0.0 copy-done.2
  64.0 0.8 shard_map.85
  64.8 21.2 %all_to_all.23 = bf16[256,4,128]{2,1,0:T(4,128)(2,1)S(1)} all-to-all(bf16[256,4,128]{2,1,0:T(4,128)(2,1)S(1)} %bitcast.14), channel_id=1, replica_groups=mesh['y'=4,'x'=4,'zh'=4,'zl'=2,'c'=2] {'zh','zl','c','y','x'}, dimensions={0} | all-to-all | bytes 524288 | tf_op jit(solution)/shard_map/all_to_all | solution.py:248
  86.0 1.1 %shard_map.86 = bf16[256,128]{1,0:T(8,128)(2,1)} custom-call(bf16[1024,128]{1,0:T(8,128)(2,1)S(1)} %bitcast.10, f32[256,128]{1,0:T(8,128)S(1)} %get-tuple-element.32.state, f32[256,128]{1,0:T(8,128)S(1)} %get-tuple-element.35.gate, bf16[256,256]{1,0:T(8,128)(2,1)S(1)} %get-tuple-element.36.spread_w), custom_call_target="tpu_custom_call" | custom-call | tf_op jit(solution)/shard_map/pallas_call | solution.py:235
Async XLA Ops:
  30.5 20.2 %copy-start.1 = (bf16[256,256]{1,0:T(8,128)(2,1)S(1)}, bf16[256,256]{1,0:T(8,128)(2,1)}, u32[]{:S(2)}) copy-start(bf16[256,256]{1,0:T(8,128)(2,1)} %constant.8.clone.deal) | copy-start | bytes 393220
  50.6 13.4 %copy-start = (bf16[2,512,256]{2,1,0:T(8,128)(2,1)S(1)}, bf16[2,512,256]{2,1,0:T(8,128)(2,1)}, u32[]{:S(2)}) copy-start(bf16[2,512,256]{2,1,0:T(8,128)(2,1)} %constant.11.clone.targets) | copy-start | bytes 1572868
  51.4 12.6 %copy-start.2 = (bf16[128,128]{1,0:T(8,128)(2,1)S(1)}, bf16[128,128]{1,0:T(8,128)(2,1)}, u32[]{:S(2)}) copy-start(bf16[128,128]{1,0:T(8,128)(2,1)} %constant.10.clone.take) | copy-start | bytes 98308

commit v8 on v5

--- a/solution.py
+++ b/solution.py
@@ -120,11 +120,9 @@
     return sent_operands(transposed(in_w, eye), normalized(state), deal), state
 
 
-def side_math(state, in_w, gate_w, out_w, eye, spread):
-    gate_t = [transposed(gate_w[u], eye) for u in range(2)]
-    out_t = [transposed(out_w[u], eye) for u in range(2)]
-    spread_w = [jnp.concatenate([moved(t, spread[r]) for r in range(2)], 0) for t in out_t]
-    return gates(gate_t[0], state), transposed(in_w, eye), gate_t[1], *spread_w
+def spread_out(weights, eye, spread):
+    weights = transposed(weights, eye)
+    return jnp.concatenate([moved(weights, spread[0:128]), moved(weights, spread[128:256])], 0)
 
 
 def outgoing_math(received, sides, rows):
@@ -139,7 +137,8 @@
     return jnp.concatenate(blocks, 0).astype(BF16)
 
 
-def middle_math(gathered, state, gate, spread_w, in_t, deal):
+def middle_math(gathered, state, gate, spread_w, in_w, deal):
+    in_t = transposed(in_w, identity())
     parts = gathered.astype(F32).reshape(2, 2, 128, 128)
     product = (parts[:, 0] + parts[:, 1]).reshape(256, 128)
     middle = residual(product, spread_w, state, gate).astype(F32)
@@ -174,11 +173,10 @@
 
 
 def first_kernel(
-    own_hbm, in_hbm, deal_hbm, gate_hbm, out_hbm,
-    sent, state, next_in, gate_w, out_w, own, in_w, deal, done,
+    own_hbm, in_hbm, gate_hbm, out_hbm, sent, state, next_in, gate_w, out_w, own, in_w, done
 ):
     routes = (
-        (own_hbm, own), (in_hbm.at[0], in_w), (deal_hbm, deal),
+        (own_hbm, own), (in_hbm.at[0], in_w),
         (in_hbm.at[1], next_in), (gate_hbm, gate_w), (out_hbm, out_w),
     )
     copies = [
@@ -187,32 +185,36 @@
     ]
     for copy in copies:
         copy.start()
-    for copy in copies[:3]:
+    row = lax.broadcasted_iota(jnp.int32, (256, 256), 0)
+    col = lax.broadcasted_iota(jnp.int32, (256, 256), 1)
+    deal = (col == row % 4 * 64 + row // 4).astype(F32).astype(BF16)
+    for copy in copies[:2]:
         copy.wait()
-    sent[...], state[...] = first_math(own[...], in_w[...], identity(), deal[...])
-    for copy in copies[3:]:
+    sent[...], state[...] = first_math(own[...], in_w[...], identity(), deal)
+    for copy in copies[2:]:
         copy.wait()
 
 
-def outgoing_kernel(
-    received, state, in_w, gate_w, out_w, moves, sent, gate, in_t, gate_t, spread_0, spread_1
+def outgoing_kernel(received, state, gate_w, out_w, moves, sent, gate, spread_w):
+    eye = identity()
+    sent[...] = outgoing_math(received[...], moves[0:256], moves[256:512])
+    gate[...] = gates(transposed(gate_w[0], eye), state[...])
+    spread_w[...] = spread_out(out_w[0], eye, moves[512:768])
+
+
+def middle_kernel(gathered, state, gate, spread_w, in_w, deal, sent, middle):
+    sent[...], middle[...] = middle_math(
+        gathered[...], state[...], gate[...], spread_w[...], in_w[...], deal[...]
+    )
+
+
+def incoming_kernel(
+    received, state, gate_w, out_w, take, targets, moves, sent, gate, spread_w
 ):
-    sent[...] = outgoing_math(received[...], moves[0:256], moves[256:512])
-    gate[...], in_t[...], gate_t[...], spread_0[...], spread_1[...] = side_math(
-        state[...], in_w[...], gate_w[...], out_w[...], identity(),
-        (moves[512:640], moves[640:768]),
-    )
-
-
-def middle_kernel(gathered, state, gate, spread_w, in_t, deal, sent, middle):
-    sent[...], middle[...] = middle_math(
-        gathered[...], state[...], gate[...], spread_w[...], in_t[...], deal[...]
-    )
-
-
-def incoming_kernel(received, state, gate_t, take, targets, sent, gate):
+    eye = identity()
     sent[...] = incoming_math(received[...], take[...], targets[...])
-    gate[...] = gates(gate_t[...], state[...])
+    gate[...] = gates(transposed(gate_w[1], eye), state[...])
+    spread_w[...] = spread_out(out_w[1], eye, moves[512:768])
 
 
 def last_kernel(gathered, state, gate, spread_w, refined):
@@ -241,7 +243,8 @@
     deal = jnp.asarray(DEAL)
     kept = ((256, 128), F32)
     wide = ((256, 256), BF16)
-    inputs = [pair_rep.reshape(256, 128), in_weights, deal, gate_weights, out_weights]
+    moves = jnp.asarray(np.concatenate([SIDES, ROWS, *SPREAD], 0))
+    inputs = [pair_rep.reshape(256, 128), in_weights, gate_weights, out_weights]
     squares = ((2, 128, 128), BF16)
     sent, state, next_in, gate_w, out_w = call(
         first_kernel, [((512, 128), BF16), kept, ((128, 512), BF16), squares, squares],
@@ -249,26 +252,25 @@
         space=pltpu.HBM,
         scratch=[
             pltpu.VMEM((256, 128), BF16), pltpu.VMEM((128, 512), BF16),
-            pltpu.VMEM((256, 256), BF16), pltpu.SemaphoreType.DMA((6,)),
+            pltpu.SemaphoreType.DMA((5,)),
         ],
     )
-    sent, gate, in_t, gate_t, spread_0, spread_1 = call(
-        outgoing_kernel,
-        [((512, 128), BF16), kept, ((512, 128), BF16), ((128, 128), BF16), wide, wide],
-        exchanged(sent, CHIPS), state, next_in, gate_w, out_w,
-        jnp.asarray(np.concatenate([SIDES, ROWS, *SPREAD], 0)),
+    sent, gate, spread_w = call(
+        outgoing_kernel, [((512, 128), BF16), kept, wide],
+        exchanged(sent, CHIPS), state, gate_w, out_w, moves,
     )
     sent, state = call(
         middle_kernel, [((512, 128), BF16), kept],
-        exchanged(sent, TO_OWNERS), state, gate, spread_0, in_t, deal,
-    )
-    sent, gate = call(
-        incoming_kernel, [((1024, 128), BF16), kept],
-        exchanged(sent, LAYER), state, gate_t, jnp.asarray(TAKE), jnp.asarray(TARGETS),
+        exchanged(sent, TO_OWNERS), state, gate, spread_w, next_in, deal,
+    )
+    sent, gate, spread_w = call(
+        incoming_kernel, [((1024, 128), BF16), kept, wide],
+        exchanged(sent, LAYER), state, gate_w, out_w,
+        jnp.asarray(TAKE), jnp.asarray(TARGETS), moves,
     )
     refined = call(
         last_kernel, [((256, 128), BF16)],
-        exchanged(sent, FROM_LAYER), state, gate, spread_1,
+        exchanged(sent, FROM_LAYER), state, gate, spread_w,
     )
     return refined.reshape(pair_rep.shape)
 

time: 86.3 us -> 86.2 us (level)
  no operation moved by 1% of the time
where the time goes in v8:
time: 86.2 us; the launch traced here: 85.9 us
  blocking collectives  80.6 us (94%)
  Pallas kernels  5.26 us (6%)
    all_to_all x4, blocking collectives, exchanged(): return lax.all_to_all(blocks, axes, 0, 0, tiled=True).reshape(rows.shape)  80.6 us
    pallas_call x5, Pallas kernels, call(): pl.pallas_call(kernel, out_shape=tuple((jax.ShapeDtypeStruct(shape, dtype...  5.26 us

profile of v8, /device:TPU:1, one launch (start us, length us, event | category | flops | bytes accessed | tf_op | source)
XLA Modules:
  0.0 85.9 jit_solution(15658554446451567254)
XLA Ops:
  0.0 0.0 copy-start
  0.0 1.7 %shard_map.82 = (bf16[512,128]{1,0:T(8,128)(2,1)S(1)}, f32[256,128]{1,0:T(8,128)S(1)}, bf16[128,512]{1,0:T(8,128)(2,1)S(1)}, bf16[2,128,128]{2,1,0:T(8,128)(2,1)S(1)}, bf16[2,128,128]{2,1,0:T(8,128)(2,1)S(1)}) custom-call(bf16[256,128]{1,0:T(8,128)(2,1)} %bitcast.18, bf16[2,128,512]{2,1,0:T(8,128)(2,1)} %in_hbm.1, bf16[2,128,128]{2,1,0:T(8,128)(2,1)} %gate_hbm.1, ...), custom_call_target="tpu_custom_call" | custom-call | tf_op jit(solution)/shard_map/pallas_call | solution.py:226
  1.7 26.5 %all_to_all.20 = bf16[128,4,128]{2,1,0:T(4,128)(2,1)S(1)} all-to-all(bf16[128,4,128]{2,1,0:T(4,128)(2,1)S(1)} %bitcast.16), channel_id=1, replica_groups=mesh['y'=4,'x'=4,'zh'=4,'zl'=2,'c'=2] {'zl','y','x','zh'}, dimensions={0} | all-to-all | bytes 262144 | tf_op jit(solution)/shard_map/all_to_all | solution.py:239
  28.2 0.0 copy-done
  28.2 0.9 %shard_map.83 = (bf16[512,128]{1,0:T(8,128)(2,1)S(1)}, f32[256,128]{1,0:T(8,128)S(1)}, bf16[256,256]{1,0:T(8,128)(2,1)S(1)}) custom-call(bf16[512,128]{1,0:T(8,128)(2,1)S(1)} %bitcast.12, f32[256,128]{1,0:T(8,128)S(1)} %get-tuple-element.19.state, bf16[2,128,128]{2,1,0:T(8,128)(2,1)S(1)} %get-tuple-element.20.gate_w, ...), custom_call_target="tpu_custom_call" | custom-call | tf_op jit(solution)/shard_map/pallas_call | solution.py:226
  29.0 0.0 copy-start.2
  29.1 19.9 %all_to_all.21 = bf16[256,2,128]{2,1,0:T(2,128)(2,1)S(1)} all-to-all(bf16[256,2,128]{2,1,0:T(2,128)(2,1)S(1)} %bitcast.17), channel_id=1, replica_groups=mesh['y'=4,'x'=4,'zh'=4,'zl'=2,'c'=2] {'zl','c','y','x','zh'}, dimensions={0} | all-to-all | bytes 262144 | tf_op jit(solution)/shard_map/all_to_all | solution.py:239
  49.0 0.0 copy-done.2
  49.0 0.0 copy-start.1
  49.0 0.8 shard_map.84
  49.7 0.0 copy-start.3
  49.7 13.1 %all_to_all.22 = bf16[64,8,128]{2,1,0:T(8,128)(2,1)S(1)} all-to-all(bf16[64,8,128]{2,1,0:T(8,128)(2,1)S(1)} %bitcast.15), channel_id=1, replica_groups=mesh['y'=4,'x'=4,'zh'=4,'zl'=2,'c'=2] {'zl','c','y','x'}, dimensions={0} | all-to-all | bytes 262144 | tf_op jit(solution)/shard_map/all_to_all | solution.py:239
  62.8 0.0 copy-done.1
  62.8 0.0 copy-done.3
  62.8 0.9 %shard_map.85 = (bf16[1024,128]{1,0:T(8,128)(2,1)S(1)}, f32[256,128]{1,0:T(8,128)S(1)}, bf16[256,256]{1,0:T(8,128)(2,1)S(1)}) custom-call(bf16[512,128]{1,0:T(8,128)(2,1)S(1)} %bitcast.13, f32[256,128]{1,0:T(8,128)S(1)} %get-tuple-element.27.state, bf16[2,128,128]{2,1,0:T(8,128)(2,1)S(1)} %get-tuple-element.20.gate_w, ...), custom_call_target="tpu_custom_call" | custom-call | tf_op jit(solution)/shard_map/pallas_call | solution.py:226
  63.7 21.2 %all_to_all.23 = bf16[256,4,128]{2,1,0:T(4,128)(2,1)S(1)} all-to-all(bf16[256,4,128]{2,1,0:T(4,128)(2,1)S(1)} %bitcast.14), channel_id=1, replica_groups=mesh['y'=4,'x'=4,'zh'=4,'zl'=2,'c'=2] {'zh','zl','c','y','x'}, dimensions={0} | all-to-all | bytes 524288 | tf_op jit(solution)/shard_map/all_to_all | solution.py:239
  84.9 1.1 %shard_map.86 = bf16[256,128]{1,0:T(8,128)(2,1)} custom-call(bf16[1024,128]{1,0:T(8,128)(2,1)S(1)} %bitcast.10, f32[256,128]{1,0:T(8,128)S(1)} %get-tuple-element.27.state, f32[256,128]{1,0:T(8,128)S(1)} %get-tuple-element.29.gate, bf16[256,256]{1,0:T(8,128)(2,1)S(1)} %get-tuple-element.30.spread_w), custom_call_target="tpu_custom_call" | custom-call | tf_op jit(solution)/shard_map/pallas_call | solution.py:226
Async XLA Ops:
  0.0 28.2 %copy-start = (bf16[768,256]{1,0:T(8,128)(2,1)S(1)}, bf16[768,256]{1,0:T(8,128)(2,1)}, u32[]{:S(2)}) copy-start(bf16[768,256]{1,0:T(8,128)(2,1)} %constant.9.clone.moves) | copy-start | bytes 1179652
  29.0 19.9 %copy-start.2 = (bf16[256,256]{1,0:T(8,128)(2,1)S(1)}, bf16[256,256]{1,0:T(8,128)(2,1)}, u32[]{:S(2)}) copy-start(bf16[256,256]{1,0:T(8,128)(2,1)} %constant.8.clone.deal) | copy-start | bytes 393220
  49.0 13.9 %copy-start.1 = (bf16[2,512,256]{2,1,0:T(8,128)(2,1)S(1)}, bf16[2,512,256]{2,1,0:T(8,128)(2,1)}, u32[]{:S(2)}) copy-start(bf16[2,512,256]{2,1,0:T(8,128)(2,1)} %constant.11.clone.targets) | copy-start | bytes 1572868
  49.7 13.1 %copy-start.3 = (bf16[128,128]{1,0:T(8,128)(2,1)S(1)}, bf16[128,128]{1,0:T(8,128)(2,1)}, u32[]{:S(2)}) copy-start(bf16[128,128]{1,0:T(8,128)(2,1)} %constant.10.clone.take) | copy-start | bytes 98308
